TPU v7x, 256 devices: a whole 4x4x8 slice. The times are simulated.
256 devices in a mesh: section: 4 (over x), tok: 32 (over z, y), head: 2 (over core).
Axes of the slice: x: 4, y: 4, z: 8, core: 2. Of those that a mesh axis runs over, the one named last changes fastest.
Arguments:
- group_in: bfloat16 [4, 4096, 2048], P('section', 'tok'), may hold values from -6 to 6
- w_qkv: bfloat16 [4, 3, 2048, 2048], P('section', None, 'tok', 'head'), may hold values from -0.125 to 0.125
- w_out: bfloat16 [4, 2048, 2048], P('section', 'head', 'tok'), may hold values from -0.125 to 0.125
- step_sizes: float32 [4, 4096, 4], P('section', 'tok', 'head'), may hold values from 0.05 to 1
- fast_weights: bfloat16 [4, 4, 3, 512, 512], P('section', 'head'), may hold values from -0.25 to 0.25
- momentum: bfloat16 [4, 4, 3, 512, 512], P('section', 'head'), may hold values from -48 to 48
- momentum_decay: float32 [4, 4], P('section', 'head'), may hold values from 0.5 to 0.95
- fast_rate: float32 [4, 4], P('section', 'head'), may hold values from 0.3 to 1
Outputs:
- handed: bfloat16 [4, 4096, 2048], P('section', 'tok', 'head')
- fast_next: bfloat16 [4, 4, 3, 512, 512], P('section', 'head')
All inputs are finite; a program needn't handle non-finite values.
Results may differ from a plain program's by a relative error of at most 0.015.
Values may be sent and summed in bfloat16 or wider, within the bound.
No kernel may reach another device: no remote copies, remote signals or barrier semaphores. Data moves between devices by JAX's collectives and lax.ppermute only.
A program may use at most 128 MiB of HBM per device.

v0:
```python
import jax
import jax.numpy as jnp
from jax import lax
from jax.experimental import pallas as pl
from jax.experimental.pallas import tpu as pltpu
from jax.sharding import Mesh
from jax.sharding import PartitionSpec as P


NS_ITERS = 2
TOK = ("z", "y")

coef_linear = 3.4445
coef_cubic = -4.775
coef_quintic = 2.0315

bf16 = jnp.bfloat16
f32 = jnp.float32


def moved(value, axis, steps):
    count = lax.axis_size(axis)
    return lax.ppermute(value, axis, [(i, (i + steps) % count) for i in range(count)])


def swapped(value):
    return lax.ppermute(value, "head", [(0, 1), (1, 0)])


def dot(a, b, ca, cb):
    return lax.dot_general(a, b, (((ca,), (cb,)), ((), ())), preferred_element_type=f32)


def kernel_call(body, outs, args, flops=0, scratch=(), limit=24):
    size = sum(a.size * a.dtype.itemsize for a in args[1:])
    return pl.pallas_call(
        body,
        out_shape=outs,
        in_specs=[pl.BlockSpec(memory_space=pltpu.SMEM)]
        + [pl.BlockSpec(memory_space=pltpu.VMEM)] * (len(args) - 1),
        out_specs=jax.tree.map(lambda _: pl.BlockSpec(memory_space=pltpu.VMEM), outs),
        scratch_shapes=list(scratch),
        compiler_params=pltpu.CompilerParams(vmem_limit_bytes=limit << 20),
        cost_estimate=pl.CostEstimate(flops=flops, bytes_accessed=size, transcendentals=0),
    )(*args)


def shape(*dims, dtype=bf16):
    return jax.ShapeDtypeStruct(dims, dtype)


def spans(t):
    return pl.ds(pl.multiple_of(t * 64, 64), 64)


def halves(t):
    return pl.ds(pl.multiple_of(t * 256, 256), 256)


def pack_body(place, w_ref, o_ref, extra_ref, *outs):
    y = place[0]
    for k, out in enumerate(outs):
        j = lax.rem(y + k, 4)
        columns = pl.ds(pl.multiple_of(j * 256, 256), 256)
        for row, component in enumerate((1, 2, 0)):
            out[row * 64 : row * 64 + 64, :] = w_ref[component, :, columns]
        out[192:256, :] = o_ref[:, columns]
        out[256:264, :] = extra_ref[lax.div(j, 2)]


def sort_body(place, a, b, c, d, key_value, query_out, steps):
    slot = 2 * lax.rem(place[0], 2) + place[2]
    for k, piece in enumerate((a, b, c, d)):
        source = lax.rem(slot + 4 - k, 4)
        rows = pl.ds(pl.multiple_of(source * 64, 64), 64)
        for i in range(2):
            key_value[i, rows, :] = piece[i * 64 : i * 64 + 64, :]
            query_out[i, rows, :] = piece[i * 64 + 128 : i * 64 + 192, :]
        steps[source] = piece[256:264, :].astype(f32)


def project_body(place, rows, *refs):
    blocks, out, stack = refs[:8], refs[8], refs[9]

    def fill(which, carry):
        for m in range(8):
            stack[which, m * 256 : m * 256 + 256, :] = blocks[m][which]
        return carry

    lax.fori_loop(0, 2, fill, 0)

    def part(i, carry):
        out[halves(i), :] = dot(rows[halves(lax.rem(i, 2)), :], stack[lax.div(i, 2)], 1, 0)
        return carry

    lax.fori_loop(0, 4, part, 0)


def query_body(place, rows, *refs):
    blocks, (query_out, out_own, sent, stack) = refs[:8], refs[8:]
    z, core = place[1], place[2]
    for m in range(8):
        stack[m * 256 : m * 256 + 256, :] = blocks[m][0]

    def part(i, carry):
        query_out[halves(i), :] = dot(rows[halves(i), :], stack[...], 1, 0)
        return carry

    lax.fori_loop(0, 2, part, 0)

    def split(t, carry):
        value = query_out[spans(t), :]
        coarse = value.astype(bf16)
        sent[spans(t), :] = coarse
        sent[spans(t + 8), :] = (value - coarse.astype(f32)).astype(bf16)
        return carry

    lax.fori_loop(0, 8, split, 0)
    for m in range(8):
        source = lax.rem(z + m, 8)
        start = lax.rem(source, 4) * 256
        kept = lax.div(source, 4) == core

        @pl.when(kept)
        def _():
            out_own[pl.ds(pl.multiple_of(start, 256), 256), :] = blocks[m][1]

        @pl.when(jnp.logical_not(kept))
        def _():
            sent[pl.ds(pl.multiple_of(start + 1024, 256), 256), :] = blocks[m][1]


def sides(own, other, first):
    return jnp.where(first, own, other), jnp.where(first, other, own)


def normed(own, other, first, epsilon):
    low, high = sides(own, other, first)
    square = jnp.sum(low * low, axis=-1, keepdims=True) + jnp.sum(high * high, axis=-1, keepdims=True)
    factor = lax.rsqrt(square / 512 + epsilon)
    return (low * factor).astype(bf16), (high * factor).astype(bf16)


def grads_body(place, pair_own, pair_other, step, weights, own_out, *refs):
    outs, (left, right, pre, whole) = refs[:7], refs[7:]
    z, core = place[1], place[2]
    first = core == 0
    half = pl.ds(pl.multiple_of(core * 256, 256), 256)

    def inputs(t, carry):
        span, down = spans(t), spans(t + 8)
        low, high = normed(pair_own[span, :], pair_other[span, :], first, 1e-06)
        left[0, span, 0:256] = low
        left[0, span, 256:512] = high
        scale = step[span, :]
        low, high = sides(pair_own[down, :], pair_other[down, :], first)
        left[1, span, 0:256] = (-(scale * low.astype(bf16).astype(f32))).astype(bf16)
        left[1, span, 256:512] = (-(scale * high.astype(bf16).astype(f32))).astype(bf16)
        return carry

    lax.fori_loop(0, 8, inputs, 0)

    def inner(i, carry):
        pre[i] = dot(left[lax.div(i, 2)], weights[i, :, half], 1, 0)
        return carry

    lax.fori_loop(0, 3, inner, 0)

    def middle(t, carry):
        span = spans(t)
        gate, up, back = pre[0, span, :], pre[1, span, :], pre[2, span, :]
        squash = jax.nn.sigmoid(gate)
        right[2, span, :] = (gate * squash * up).astype(bf16)
        right[0, span, :] = (back * up * squash * (1.0 + gate * (1.0 - squash))).astype(bf16)
        right[1, span, :] = (back * gate * squash).astype(bf16)
        return carry

    lax.fori_loop(0, 8, middle, 0)

    def outer(i, carry):
        whole[i] = dot(left[lax.div(i, 2)], right[i], 0, 0)
        for m in range(8):
            value = whole[i, spans(lax.rem(z + m, 8)), :]
            if m == 0:
                own_out[spans(i), :] = value
            else:
                outs[m - 1][spans(i), :] = value.astype(bf16)
        return carry

    lax.fori_loop(0, 3, outer, 0)


def order_body(place, *refs):
    for m in range(8):
        for i in range(3):
            refs[9][spans(i * 8 + lax.rem(place[1] + m, 8)), :] = refs[m][i * 64 : i * 64 + 64, :]

    def tile(t, carry):
        refs[9][spans(t + 24), :] = refs[8][spans(t), :]
        return carry

    lax.fori_loop(0, 32, tile, 0)


def newton_body(place, own, other, weights, rate, out, x_ref):
    first = place[2] == 0

    def start(m, carry):
        def square(t, total):
            low, high = own[spans(m * 8 + t), :].astype(f32), other[spans(m * 8 + t), :].astype(f32)
            return total + low * low + high * high

        total = jnp.sum(lax.fori_loop(0, 8, square, jnp.zeros((64, 256), f32)))
        factor = 1.0 / (jnp.sqrt(jnp.full((1, 1), total)) + 1e-06)

        def scale(t, inner):
            low, high = sides(own[spans(m * 8 + t), :], other[spans(m * 8 + t), :], first)
            x_ref[m, spans(t), 0:256] = (low.astype(f32) * factor).astype(bf16)
            x_ref[m, spans(t), 256:512] = (high.astype(f32) * factor).astype(bf16)
            return inner

        return lax.fori_loop(0, 8, scale, carry)

    lax.fori_loop(0, 3, start, 0)

    def iteration(i, carry):
        m = lax.rem(i, 3)
        x = x_ref[m]
        gram = dot(x, x, 0, 0).astype(bf16)
        cubic = dot(x, gram, 1, 0)
        quintic = dot(cubic.astype(bf16), gram, 1, 0)
        x_ref[m] = (
            coef_linear * x.astype(f32) + coef_cubic * cubic + coef_quintic * quintic
        ).astype(bf16)
        return carry

    lax.fori_loop(0, 3 * NS_ITERS, iteration, 0)

    def update(i, carry):
        m, span = lax.div(i, 8), spans(lax.rem(i, 8))
        change = rate[0, 0] * x_ref[m, span, :].astype(f32)
        out[m, span, :] = (weights[m, span, :].astype(f32) - change).astype(bf16)
        return carry

    lax.fori_loop(0, 24, update, 0)


def apply_body(place, query_own, out_own, other, updated, out, top, bottom, *refs):
    query, pre_ref, hidden, mixed, left_ref, right_ref, full = refs
    first = place[2] == 0

    def inputs(t, carry):
        span = spans(t)
        arrived = other[spans(t + 24), :].astype(f32) + other[spans(t + 32), :].astype(f32)
        low, high = normed(query_own[span, :], arrived, first, 1e-06)
        query[span, 0:256] = low
        query[span, 256:512] = high
        return carry

    lax.fori_loop(0, 8, inputs, 0)

    def inner(i, carry):
        part = halves(lax.rem(i, 2))
        pre_ref[lax.div(i, 2), part, :] = dot(query[part, :], updated[lax.div(i, 2)], 1, 0)
        return carry

    lax.fori_loop(0, 4, inner, 0)

    def middle(t, carry):
        gate = pre_ref[0, spans(t), :]
        hidden[spans(t), :] = (gate * jax.nn.sigmoid(gate) * pre_ref[1, spans(t), :]).astype(bf16)
        return carry

    lax.fori_loop(0, 8, middle, 0)

    def outer(i, carry):
        mixed[halves(i), :] = dot(hidden[halves(i), :], updated[2], 1, 1)
        return carry

    lax.fori_loop(0, 2, outer, 0)

    def scaled(t, carry):
        value = mixed[spans(t), :]
        value = value * lax.rsqrt(jnp.mean(value * value, axis=-1, keepdims=True) + 1e-05)
        left, right = sides(value[:, 0:256], value[:, 256:512], first)
        left_ref[spans(t), :] = left.astype(bf16)
        right_ref[spans(t), :] = right.astype(bf16)
        return carry

    lax.fori_loop(0, 8, scaled, 0)

    def last(i, carry):
        full[i] = dot(left_ref[...], out_own[halves(i), :], 1, 1) + dot(
            right_ref[...], other[halves(i + 10), :], 1, 1
        )
        columns = halves(i)
        out[:, columns] = full[i, 0:384, :]
        top[:, columns] = full[i, 384:448, :].astype(bf16)
        bottom[:, columns] = full[i, 448:512, :].astype(bf16)
        return carry

    lax.fori_loop(0, 4, last, 0)


def relay_body(place, partial, top, bottom, low_out, high_out):
    low_out[0:64, :] = partial[128:192, :].astype(bf16)
    low_out[64:128, :] = (partial[192:256, :] + bottom[...].astype(f32)).astype(bf16)
    high_out[0:64, :] = (partial[256:320, :] + top[...].astype(f32)).astype(bf16)
    high_out[64:128, :] = partial[320:384, :].astype(bf16)


def payload_body(place, weights, momentum, scalars, out):
    def tile(i, carry):
        out[spans(i), :] = weights[lax.rem(place[0], 2), lax.div(i, 8), spans(lax.rem(i, 8)), :]
        return carry

    lax.fori_loop(0, 24, tile, 0)
    out[1536:1728, :] = momentum[...]
    out[1728:1736, :] = scalars[...]


def choose_body(place, mine, arrived, weights_out, momentum_out, scalars_out):
    owner = lax.div(place[0], 2) == place[2]
    columns = pl.ds(pl.multiple_of(place[2] * 256, 256), 256)

    def take(source):
        def tile(i, carry):
            weights_out[lax.div(i, 8), spans(lax.rem(i, 8)), :] = source[spans(i), :]
            return carry

        lax.fori_loop(0, 24, tile, 0)
        momentum_out[...] = source[1536:1728, columns].astype(f32)
        scalars_out[...] = source[1728:1736, :].astype(f32)

    @pl.when(owner)
    def _():
        take(mine)

    @pl.when(jnp.logical_not(owner))
    def _():
        take(arrived)


def copies(moves, sems):
    started = [pltpu.make_async_copy(a, b, sems.at[i]) for i, (a, b) in enumerate(moves)]
    for copy in started:
        copy.start()
    for copy in started:
        copy.wait()


def emit_body(place, made, across, outward, out, sems):
    slot = lax.rem(place[0], 2)
    owner = lax.div(place[0], 2) == place[2]

    @pl.when(owner)
    def _():
        copies([(made, out.at[slot]), (across, out.at[1 - slot])], sems)

    @pl.when(jnp.logical_not(owner))
    def _():
        copies([(outward, out.at[1 - slot])], sems)


def finish_body(place, relayed, traded, _, out, sems):
    slot = lax.rem(place[0], 2)

    @pl.when(lax.div(place[0], 2) != place[2])
    def _():
        moves = [
            (relayed, out.at[slot, :, pl.ds(0, 256)]),
            (traded, out.at[slot, :, pl.ds(256, 256)]),
        ]
        copies(moves, sems)


def turn_body(place, tokens, out):
    for m in range(8):
        start = pl.multiple_of(lax.rem(place[1] + m, 8) * 256, 256)
        out[:, m * 256 : m * 256 + 256] = tokens[:, pl.ds(start, 256)]


def total_body(place, tokens, partial, low, high, out):
    columns = pl.ds(pl.multiple_of(place[2] * 1024, 1024), 1024)

    def tile(t, carry):
        span = pl.ds(pl.multiple_of(t * 16, 16), 16)
        total = tokens[span, columns].astype(f32) + partial[span, :]
        out[span, :] = (total + low[span, :].astype(f32) + high[span, :].astype(f32)).astype(bf16)
        return carry

    lax.fori_loop(0, 8, tile, 0)


def to_head_chips(pieces):
    got = []
    for k, part in enumerate(pieces):
        pairs = []
        for source in range(4):
            for c in range(2):
                j = (source + k) % 4
                pairs.append((source * 2 + c, (2 * c + j // 2) * 2 + j % 2))
        got.append(lax.ppermute(part, ("y", "head"), pairs))
    return got


def ring_gather(chunk, ups, downs):
    up, down = [chunk], [chunk]
    for step in range(4):
        if step < ups:
            up.append(moved(up[-1], "z", 1))
        if step < downs:
            down.append(moved(down[-1], "z", -1))
    return down + up[:0:-1]


def section_step(group_in, w_qkv, w_out, step_sizes, fast_weights, momentum, momentum_decay, fast_rate):
    core, y, z = lax.axis_index("head"), lax.axis_index("y"), lax.axis_index("z")
    place = jnp.stack([y, z, core])

    steps = step_sizes[0].T
    steps_high = lax.reduce_precision(steps, 8, 7)
    extra = jnp.concatenate([steps_high, steps - steps_high], axis=1).astype(bf16)
    extra = jnp.broadcast_to(extra[:, None, :], (2, 8, 256))
    pieces = kernel_call(pack_body, [shape(264, 256)] * 4, [place, w_qkv[0], w_out[0].T, extra])
    key_value, query_out, step_rows = kernel_call(
        sort_body,
        [shape(2, 256, 256), shape(2, 256, 256), shape(4, 8, 256, dtype=f32)],
        [place, *to_head_chips(pieces)],
    )

    key_value_blocks = ring_gather(key_value, 4, 3)
    query_out_blocks = ring_gather(query_out, 3, 4)

    step_all = step_rows[:, 0, :128] + step_rows[:, 0, 128:]
    step = jnp.concatenate(
        [lax.dynamic_index_in_dim(step_all, (y + k) % 4, 0, False) for k in (0, 3, 1, 2)]
    )[:, None]

    tokens, _ = lax.optimization_barrier((group_in[0], pieces[0]))
    turned = kernel_call(turn_body, shape(128, 2048), [place, tokens])
    rows = jnp.concatenate(
        [turned, moved(turned, "y", 1), moved(turned, "y", -1), moved(turned, "y", 2)]
    )

    part = lax.dynamic_slice(momentum[0], (y % 2, 0, z * 64, 0), (1, 3, 64, 512)).reshape(192, 512)
    scalars = jnp.stack([momentum_decay[0], fast_rate[0]])
    scalars = lax.dynamic_index_in_dim(scalars, y % 2, 1, False)
    terms = []
    for _ in range(3):
        term = lax.reduce_precision(scalars, 8, 7)
        terms.append(term)
        scalars = scalars - term
    terms = jnp.pad(jnp.concatenate(terms), (0, 2))
    terms = jnp.broadcast_to(terms[:, None], (8, 512)).astype(bf16)
    part, terms, _ = lax.optimization_barrier((part, terms, pieces[0]))
    mine = kernel_call(payload_body, shape(1736, 512), [place, fast_weights[0], part, terms])
    pairs = [(yy * 2 + yy // 2, yy * 2 + 1 - yy // 2) for yy in range(4)]
    mine_sent = lax.ppermute(mine, ("y", "head"), pairs)
    weights, momentum_own, terms = kernel_call(
        choose_body,
        [shape(3, 512, 512), shape(192, 256, dtype=f32), shape(8, 512, dtype=f32)],
        [place, mine, mine_sent],
    )
    decay = terms[0, 0] + terms[2, 0] + terms[4, 0]
    rate = (terms[1, 0] + terms[3, 0] + terms[5, 0]).reshape(1, 1)

    pair = kernel_call(
        project_body,
        shape(1024, 256, dtype=f32),
        [place, rows, *key_value_blocks],
        flops=2 * 512 * 2048 * 512,
        scratch=[pltpu.VMEM((2, 2048, 256), bf16)],
    )
    pair_other = swapped(pair)
    own_sum, *parts = kernel_call(
        grads_body,
        [shape(192, 256, dtype=f32)] + [shape(192, 256)] * 7,
        [place, pair, pair_other, step, weights],
        flops=2 * 512 * 512 * 256 * 6,
        scratch=[
            pltpu.VMEM((2, 512, 512), bf16),
            pltpu.VMEM((3, 512, 256), bf16),
            pltpu.VMEM((3, 512, 256), f32),
            pltpu.VMEM((3, 512, 256), f32),
        ],
    )
    to_up = moved(parts[3 - 1], "z", 1)
    to_far = moved(parts[4 - 1], "z", 2)
    to_down = moved(parts[5 - 1], "z", -1)
    near = [moved(parts[1 - 1], "z", 1), moved(parts[7 - 1], "z", -1)]
    ahead = (parts[2 - 1].astype(f32) + to_up.astype(f32) + to_far.astype(f32)).astype(bf16)
    behind = (parts[6 - 1].astype(f32) + to_down.astype(f32)).astype(bf16)
    rows, _ = lax.optimization_barrier((rows, parts[3]))
    query_half, out_own, query_sent = kernel_call(
        query_body,
        [shape(512, 256, dtype=f32), shape(1024, 256), shape(2048, 256)],
        [place, rows, *query_out_blocks],
        flops=2 * 512 * 2048 * 256,
        scratch=[pltpu.VMEM((2048, 256), bf16)],
    )
    own_sum, _ = lax.optimization_barrier((own_sum, query_sent))
    total = own_sum
    for term in (*near, moved(ahead, "z", 2), moved(behind, "z", -2)):
        total = total + term.astype(f32)
    moment = (decay * momentum_own + total).astype(bf16)
    around = {0: moment, 2: moved(moment, "z", -2), 6: moved(moment, "z", 2)}
    around[1], around[7] = moved(moment, "z", -1), moved(moment, "z", 1)
    around[3], around[5] = moved(around[2], "z", -1), moved(around[6], "z", 1)
    around[4] = moved(around[2], "z", -2)
    moment_half = kernel_call(
        order_body, shape(3584, 256), [place] + [around[m] for m in range(8)] + [query_sent]
    )

    moment_other = swapped(moment_half)
    made = kernel_call(
        newton_body,
        shape(3, 512, 512),
        [place, moment_half, moment_other, weights, rate],
        flops=2 * 512**3 * 18,
        scratch=[pltpu.VMEM((3, 512, 512), bf16)],
    )

    def along(value, hops):
        return lax.ppermute(value, ("y", "head"), [(a * 2 + c, b * 2 + d) for a, c, b, d in hops])

    outer = [(1, 2), (0, 3), (3, 0), (2, 1)]
    across = along(made, [(a, a // 2, a ^ 1, a // 2) for a in range(4)])
    outward = along(made, [(a, a // 2, b, a // 2) for a, b in outer])

    partial, top, bottom = kernel_call(
        apply_body,
        [shape(384, 1024, dtype=f32), shape(64, 1024), shape(64, 1024)],
        [place, query_half, out_own, moment_other, made],
        flops=2 * 512**3 * 5,
        scratch=[
            pltpu.VMEM((512, 512), bf16),
            pltpu.VMEM((2, 512, 512), f32),
            pltpu.VMEM((512, 512), bf16),
            pltpu.VMEM((512, 512), f32),
            pltpu.VMEM((512, 256), bf16),
            pltpu.VMEM((512, 256), bf16),
            pltpu.VMEM((4, 512, 256), f32),
        ],
    )
    low, high = kernel_call(
        relay_body,
        [shape(128, 1024)] * 2,
        [place, partial, moved(top, "y", 1), moved(bottom, "y", -1)],
    )
    across, outward, _ = lax.optimization_barrier((across, outward, low))
    relayed = along(across[:, :256], [(a, a // 2, b, a // 2) for a, b in outer])
    traded = along(outward[:, 256:], [(a, 1 - a // 2, a ^ 1, 1 - a // 2) for a in range(4)])

    def emit(body, values, **more):
        count = len(values)
        return pl.pallas_call(
            body,
            out_shape=shape(2, 3, 512, 512),
            in_specs=[pl.BlockSpec(memory_space=pltpu.SMEM)]
            + [pl.BlockSpec(memory_space=pltpu.VMEM)] * count
            + [pl.BlockSpec(memory_space=pl.ANY)] * (len(more) > 0),
            out_specs=pl.BlockSpec(memory_space=pl.ANY),
            scratch_shapes=[pltpu.SemaphoreType.DMA((2,))],
            compiler_params=pltpu.CompilerParams(vmem_limit_bytes=16 << 20),
            cost_estimate=pl.CostEstimate(flops=0, bytes_accessed=3 << 20, transcendentals=0),
            **({"input_output_aliases": {count + 1: 0}} if more else {}),
        )(place, *values, *more.values())

    fast_next = emit(emit_body, (made, across, outward))
    fast_next = emit(finish_body, (relayed, traded), base=fast_next)
    sent_low, sent_high = moved(low, "y", -1), moved(high, "y", 1)
    layer_out = kernel_call(
        total_body, shape(128, 1024), [place, group_in[0], partial, sent_low, sent_high]
    )
    handed = moved(layer_out[None], "section", 1)
    return (handed, fast_next[None])


def solution(mesh):
    torus = Mesh(
        mesh.devices.reshape(mesh.shape["section"], 8, 4, mesh.shape["head"]),
        ("section", "z", "y", "head"),
    )
    return jax.shard_map(
        section_step,
        mesh=torus,
        in_specs=(
            P("section", TOK, None),
            P("section", None, TOK, "head"),
            P("section", "head", TOK),
            P("section", TOK, "head"),
            P("section", "head", None, None, None),
            P("section", "head", None, None, None),
            P("section", "head"),
            P("section", "head"),
        ),
        out_specs=(P("section", TOK, "head"), P("section", "head", None, None, None)),
        check_vma=False,
    )
```

profile of v0, /device:TPU:1, one launch (start us, length us, event | category | flops | bytes accessed | tf_op | source)
XLA Modules:
  0.0 213.4 jit_solution(12190007658866261185)
XLA Ops:
  4.2 6.2 %collective-permute-start.3 = (bf16[264,256]{1,0:T(8,128)(2,1)S(1)}, bf16[264,256]{1,0:T(8,128)(2,1)S(1)}, u32[]{:S(2)}, u32[]{:S(2)}) collective-permute-start(bf16[264,256]{1,0:T(8,128)(2,1)S(1)} %get-tuple-element.35), channel_id=1, source_target_pairs={{0,0},{1,4},{2,1},{3,5},{4,2},{5,6},{6,3},{7,7},{8,8},{9,12},{10,9... | collective-permute-start | bytes 405512 | tf_op jit(solution)/shard_map/ppermute | solution.py:403
  10.4 2.9 %collective-permute-start.4 = (bf16[264,256]{1,0:T(8,128)(2,1)S(1)}, bf16[264,256]{1,0:T(8,128)(2,1)S(1)}, u32[]{:S(2)}, u32[]{:S(2)}) collective-permute-start(bf16[264,256]{1,0:T(8,128)(2,1)S(1)} %get-tuple-element.37), channel_id=1, source_target_pairs={{0,1},{1,5},{2,2},{3,6},{4,3},{5,7},{6,0},{7,4},{8,9},{9,13},{10,1... | collective-permute-start | bytes 405512 | tf_op jit(solution)/shard_map/ppermute | solution.py:403
  25.2 4.0 %collective-permute-start.7 = (bf16[2,256,256]{2,1,0:T(8,128)(2,1)}, bf16[2,256,256]{2,1,0:T(8,128)(2,1)}, u32[]{:S(2)}, u32[]{:S(2)}) collective-permute-start(bf16[2,256,256]{2,1,0:T(8,128)(2,1)} %get-tuple-element.40.refs_0_), channel_id=1, source_target_pairs={{0,56},{8,0},{16,8},{24,16},{32,24},{40,32},{48,40},{56,48},{1,57}... | collective-permute-start | bytes 786440 | tf_op jit(solution)/shard_map/ppermute | solution.py:23
  29.3 5.3 %collective-permute-done.10.refs_7_ = bf16[2,256,256]{2,1,0:T(8,128)(2,1)} collective-permute-done((bf16[2,256,256]{2,1,0:T(8,128)(2,1)}, bf16[2,256,256]{2,1,0:T(8,128)(2,1)}, u32[]{:S(2)}, u32[]{:S(2)}) %collective-permute-start.10) | collective-permute-done | bytes 262176 | tf_op jit(solution)/shard_map/ppermute | solution.py:23
  42.9 3.6 %collective-permute-done.8.refs_2_ = bf16[2,256,256]{2,1,0:T(8,128)(2,1)S(1)} collective-permute-done((bf16[2,256,256]{2,1,0:T(8,128)(2,1)}, bf16[2,256,256]{2,1,0:T(8,128)(2,1)S(1)}, u32[]{:S(2)}, u32[]{:S(2)}) %collective-permute-start.8) | collective-permute-done | bytes 262176 | tf_op jit(solution)/shard_map/ppermute | solution.py:23
  46.5 3.4 %collective-permute-start.9 = (bf16[2,256,256]{2,1,0:T(8,128)(2,1)S(1)}, bf16[2,256,256]{2,1,0:T(8,128)(2,1)S(1)}, u32[]{:S(2)}, u32[]{:S(2)}) collective-permute-start(bf16[2,256,256]{2,1,0:T(8,128)(2,1)S(1)} %collective-permute-done.8.refs_2_), channel_id=1, source_target_pairs={{0,56},{8,0},{16,8},{24,16},{32,24},{40,32},{48,40},{56,48},{1,57}... | collective-permute-start | bytes 786440 | tf_op jit(solution)/shard_map/ppermute | solution.py:23
  53.2 3.2 %collective-permute-done.13.refs_4_ = bf16[2,256,256]{2,1,0:T(8,128)(2,1)S(1)} collective-permute-done((bf16[2,256,256]{2,1,0:T(8,128)(2,1)S(1)}, bf16[2,256,256]{2,1,0:T(8,128)(2,1)S(1)}, u32[]{:S(2)}, u32[]{:S(2)}) %collective-permute-start.13) | collective-permute-done | bytes 262176 | tf_op jit(solution)/shard_map/ppermute | solution.py:23
  56.4 4.1 %shard_map.98.pair_own = f32[1024,256]{1,0:T(8,128)} custom-call(s32[3]{0:T(128)S(1)} %pad_add_fusion.place, bf16[512,2048]{1,0:T(8,128)(2,1)S(1)} %pad_maximum_fusion.rows, bf16[2,256,256]{2,1,0:T(8,128)(2,1)} %get-tuple-element.40.refs_0_, bf16[2,256,256]{2,1,0:T(8,128)(2,1)} %collective-permute-done.7.refs_1_, ...), custom_call_target="tpu_custom_call" | custom-call | flops 1073741824 | bytes 4194304 | tf_op jit(solution)/shard_map/pallas_call | solution.py:36
  60.5 5.5 %collective-permute-start.14 = (f32[1024,256]{1,0:T(8,128)}, f32[1024,256]{1,0:T(8,128)}, u32[]{:S(2)}, u32[]{:S(2)}) collective-permute-start(f32[1024,256]{1,0:T(8,128)} %shard_map.98.pair_own), channel_id=1, source_target_pairs={{0,1},{1,0},{2,3},{3,2},{4,5},{5,4},{6,7},{7,6},{8,9},{9,8},{10,11... | collective-permute-start | bytes 3145736 | tf_op jit(solution)/shard_map/ppermute | solution.py:27
  67.5 6.4 %collective-permute-done.16.refs_1_ = bf16[2,256,256]{2,1,0:T(8,128)(2,1)} collective-permute-done((bf16[2,256,256]{2,1,0:T(8,128)(2,1)S(1)}, bf16[2,256,256]{2,1,0:T(8,128)(2,1)}, u32[]{:S(2)}, u32[]{:S(2)}) %collective-permute-start.16) | collective-permute-done | bytes 262176 | tf_op jit(solution)/shard_map/ppermute | solution.py:23
  75.5 5.7 %collective-permute-done.17.refs_2_ = bf16[2,256,256]{2,1,0:T(8,128)(2,1)} collective-permute-done((bf16[2,256,256]{2,1,0:T(8,128)(2,1)}, bf16[2,256,256]{2,1,0:T(8,128)(2,1)}, u32[]{:S(2)}, u32[]{:S(2)}) %collective-permute-start.17) | collective-permute-done | bytes 262176 | tf_op jit(solution)/shard_map/ppermute | solution.py:23
  81.2 3.0 %collective-permute-start.18 = (bf16[2,256,256]{2,1,0:T(8,128)(2,1)}, bf16[2,256,256]{2,1,0:T(8,128)(2,1)}, u32[]{:S(2)}, u32[]{:S(2)}) collective-permute-start(bf16[2,256,256]{2,1,0:T(8,128)(2,1)} %collective-permute-done.17.refs_2_), channel_id=1, source_target_pairs={{0,56},{8,0},{16,8},{24,16},{32,24},{40,32},{48,40},{56,48},{1,57}... | collective-permute-start | bytes 786440 | tf_op jit(solution)/shard_map/ppermute | solution.py:23
  86.7 5.2 %shard_map.101 = (f32[192,256]{1,0:T(8,128)S(1)}, bf16[192,256]{1,0:T(8,128)(2,1)S(1)}, bf16[192,256]{1,0:T(8,128)(2,1)S(1)}, bf16[192,256]{1,0:T(8,128)(2,1)S(1...) custom-call(s32[3]{0:T(128)S(1)} %pad_add_fusion.place, ...), custom_call_target="tpu_custom_call" | custom-call | flops 805306368 | bytes 3672064 | tf_op jit(solution)/shard_map/pallas_call | solution.py:36
  101.0 3.8 %collective-permute-done.28 = bf16[192,256]{1,0:T(8,128)(2,1)S(1)} collective-permute-done((bf16[192,256]{1,0:T(8,128)(2,1)S(1)}, bf16[192,256]{1,0:T(8,128)(2,1)S(1)}, u32[]{:S(2)}, u32[]{:S(2)}) %collective-permute-start.28) | collective-permute-done | bytes 98336 | tf_op jit(solution)/shard_map/ppermute | solution.py:23
  113.6 2.8 %collective-permute-start.31 = (bf16[192,256]{1,0:T(8,128)(2,1)S(1)}, bf16[192,256]{1,0:T(8,128)(2,1)S(1)}, u32[]{:S(2)}, u32[]{:S(2)}) collective-permute-start(bf16[192,256]{1,0:T(8,128)(2,1)S(1)} %add_convert_fusion.refs_0_), channel_id=1, source_target_pairs={{0,48},{8,56},{16,0},{24,8},{32,16},{40,24},{48,32},{56,40},{1,49}... | collective-permute-start | bytes 294920 | tf_op jit(solution)/shard_map/ppermute | solution.py:23
  123.8 5.2 %collective-permute-done.33.refs_4_ = bf16[192,256]{1,0:T(8,128)(2,1)S(1)} collective-permute-done((bf16[192,256]{1,0:T(8,128)(2,1)S(1)}, bf16[192,256]{1,0:T(8,128)(2,1)S(1)}, u32[]{:S(2)}, u32[]{:S(2)}) %collective-permute-start.33) | collective-permute-done | bytes 98336 | tf_op jit(solution)/shard_map/ppermute | solution.py:23
  129.8 8.2 %collective-permute-start.37 = (bf16[3584,256]{1,0:T(8,128)(2,1)S(1)}, bf16[3584,256]{1,0:T(8,128)(2,1)S(1)}, u32[]{:S(2)}, u32[]{:S(2)}) collective-permute-start(bf16[3584,256]{1,0:T(8,128)(2,1)S(1)} %shard_map.103.own), channel_id=1, source_target_pairs={{0,1},{1,0},{2,3},{3,2},{4,5},{5,4},{6,7},{7,6},{8,9},{9,8},{10,11... | collective-permute-start | bytes 5505032 | tf_op jit(solution)/shard_map/ppermute | solution.py:27
  141.4 10.0 %shard_map.104.updated.made = bf16[3,512,512]{2,1,0:T(8,128)(2,1)S(1)} custom-call(s32[3]{0:T(128)S(1)} %pad_add_fusion.place, bf16[3584,256]{1,0:T(8,128)(2,1)S(1)} %shard_map.103.own, bf16[3584,256]{1,0:T(8,128)(2,1)S(1)} %collective-permute-done.37.other, bf16[3,512,512]{2,1,0:T(8,128)(2,1)S(1)} %get-tuple-element.44.weights, f32[1,1]{1,0:T(1,128)S(6)} %add.122.rate), custom_call_target="tpu_custom_call" | custom-call | flops 4831838208 | bytes 5242884 | tf_op jit(solution)/shard_map/pallas_call | solution.py:36
  153.5 5.8 %shard_map.105 = (f32[384,1024]{1,0:T(8,128)S(1)}, bf16[64,1024]{1,0:T(8,128)(2,1)S(1)}, bf16[64,1024]{1,0:T(8,128)(2,1)S(1)}) custom-call(s32[3]{0:T(128)S(1)} %pad_add_fusion.place, f32[512,256]{1,0:T(8,128)S(1)} %get-tuple-element.48.query_own, bf16[1024,256]{1,0:T(8,128)(2,1)S(1)} %get-tuple-element.49.out_own, ...), custom_call_target="tpu_custom_call" | custom-call | flops 1342177280 | bytes 4456448 | tf_op jit(solution)/shard_map/pallas_call | solution.py:36
  159.6 5.6 %collective-permute-start.39 = (bf16[64,1024]{1,0:T(8,128)(2,1)S(1)}, bf16[64,1024]{1,0:T(8,128)(2,1)S(1)}, u32[]{:S(2)}, u32[]{:S(2)}) collective-permute-start(bf16[64,1024]{1,0:T(8,128)(2,1)S(1)} %get-tuple-element.63), channel_id=1, source_target_pairs={{0,6},{2,0},{4,2},{6,4},{1,7},{3,1},{5,3},{7,5},{8,14},{10,8},{12,... | collective-permute-start | bytes 393224 | tf_op jit(solution)/shard_map/ppermute | solution.py:23
  165.2 14.5 %collective-permute-done.38.top = bf16[64,1024]{1,0:T(8,128)(2,1)S(1)} collective-permute-done((bf16[64,1024]{1,0:T(8,128)(2,1)S(1)}, bf16[64,1024]{1,0:T(8,128)(2,1)S(1)}, u32[]{:S(2)}, u32[]{:S(2)}) %collective-permute-start.38) | collective-permute-done | bytes 131104 | tf_op jit(solution)/shard_map/ppermute | solution.py:23
  181.8 2.8 %collective-permute-start.46 = (bf16[3,256,512]{2,1,0:T(8,128)(2,1)S(1)}, bf16[3,256,512]{2,1,0:T(8,128)(2,1)S(1)}, u32[]{:S(2)}, u32[]{:S(2)}) collective-permute-start(bf16[3,256,512]{2,1,0:T(8,128)(2,1)S(1)} %slice.39), channel_id=1, source_target_pairs={{1,3},{3,1},{4,6},{6,4},{9,11},{11,9},{12,14},{14,12},{17,19},{19,... | collective-permute-start | bytes 2359304 | tf_op jit(solution)/shard_map/ppermute | solution.py:525
  186.1 14.0 %collective-permute-done.40.low = bf16[128,1024]{1,0:T(8,128)(2,1)S(1)} collective-permute-done((bf16[128,1024]{1,0:T(8,128)(2,1)S(1)}, bf16[128,1024]{1,0:T(8,128)(2,1)S(1)}, u32[]{:S(2)}, u32[]{:S(2)}) %collective-permute-start.40) | collective-permute-done | bytes 262176 | tf_op jit(solution)/shard_map/ppermute | solution.py:23
  202.2 7.1 %collective-permute-done.42 = bf16[1,128,1024]{2,1,0:T(8,128)(2,1)S(1)} collective-permute-done((bf16[1,128,1024]{2,1,0:T(8,128)(2,1)S(1)}, bf16[1,128,1024]{2,1,0:T(8,128)(2,1)S(1)}, u32[]{:S(2)}, u32[]{:S(2)}) %collective-permute-start.42) | collective-permute-done | bytes 262176 | tf_op jit(solution)/shard_map/ppermute | solution.py:23
  (131 shorter events, 70.1 us)
Async XLA Ops:
  4.2 15.9 %collective-permute-start.3 = (bf16[264,256]{1,0:T(8,128)(2,1)S(1)}, bf16[264,256]{1,0:T(8,128)(2,1)S(1)}, u32[]{:S(2)}, u32[]{:S(2)}) collective-permute-start(bf16[264,256]{1,0:T(8,128)(2,1)S(1)} %get-tuple-element.35), channel_id=1, source_target_pairs={{0,0},{1,4},{2,1},{3,5},{4,2},{5,6},{6,3},{7,7},{8,8},{9,12},{10,9... | collective-permute-start | bytes 405512 | tf_op jit(solution)/shard_map/ppermute | solution.py:403
  10.4 10.4 %collective-permute-start.4 = (bf16[264,256]{1,0:T(8,128)(2,1)S(1)}, bf16[264,256]{1,0:T(8,128)(2,1)S(1)}, u32[]{:S(2)}, u32[]{:S(2)}) collective-permute-start(bf16[264,256]{1,0:T(8,128)(2,1)S(1)} %get-tuple-element.37), channel_id=1, source_target_pairs={{0,1},{1,5},{2,2},{3,6},{4,3},{5,7},{6,0},{7,4},{8,9},{9,13},{10,1... | collective-permute-start | bytes 405512 | tf_op jit(solution)/shard_map/ppermute | solution.py:403
  18.0 22.1 %collective-permute-start = (bf16[128,2048]{1,0:T(8,128)(2,1)}, bf16[128,2048]{1,0:T(8,128)(2,1)}, u32[]{:S(2)}, u32[]{:S(2)}) collective-permute-start(bf16[128,2048]{1,0:T(8,128)(2,1)} %shard_map.96), channel_id=1, source_target_pairs={{0,2},{2,4},{4,6},{6,0},{1,3},{3,5},{5,7},{7,1},{8,10},{10,12},{12... | collective-permute-start | bytes 1572872 | tf_op jit(solution)/shard_map/ppermute | solution.py:23
  20.1 29.9 %collective-permute-start.1 = (bf16[128,2048]{1,0:T(8,128)(2,1)}, bf16[128,2048]{1,0:T(8,128)(2,1)}, u32[]{:S(2)}, u32[]{:S(2)}) collective-permute-start(bf16[128,2048]{1,0:T(8,128)(2,1)} %shard_map.96), channel_id=1, source_target_pairs={{0,6},{2,0},{4,2},{6,4},{1,7},{3,1},{5,3},{7,5},{8,14},{10,8},{12,... | collective-permute-start | bytes 1572872 | tf_op jit(solution)/shard_map/ppermute | solution.py:23
  20.8 29.1 %collective-permute-start.2 = (bf16[128,2048]{1,0:T(8,128)(2,1)}, bf16[128,2048]{1,0:T(8,128)(2,1)}, u32[]{:S(2)}, u32[]{:S(2)}) collective-permute-start(bf16[128,2048]{1,0:T(8,128)(2,1)} %shard_map.96), channel_id=1, source_target_pairs={{0,4},{2,6},{4,0},{6,2},{1,5},{3,7},{5,1},{7,3},{8,12},{10,14},{12... | collective-permute-start | bytes 1572872 | tf_op jit(solution)/shard_map/ppermute | solution.py:23
  23.4 11.2 %collective-permute-start.10 = (bf16[2,256,256]{2,1,0:T(8,128)(2,1)}, bf16[2,256,256]{2,1,0:T(8,128)(2,1)}, u32[]{:S(2)}, u32[]{:S(2)}) collective-permute-start(bf16[2,256,256]{2,1,0:T(8,128)(2,1)} %get-tuple-element.40.refs_0_), channel_id=1, source_target_pairs={{0,8},{8,16},{16,24},{24,32},{32,40},{40,48},{48,56},{56,0},{1,9},... | collective-permute-start | bytes 786440 | tf_op jit(solution)/shard_map/ppermute | solution.py:23
  25.2 13.6 %collective-permute-start.7 = (bf16[2,256,256]{2,1,0:T(8,128)(2,1)}, bf16[2,256,256]{2,1,0:T(8,128)(2,1)}, u32[]{:S(2)}, u32[]{:S(2)}) collective-permute-start(bf16[2,256,256]{2,1,0:T(8,128)(2,1)} %get-tuple-element.40.refs_0_), channel_id=1, source_target_pairs={{0,56},{8,0},{16,8},{24,16},{32,24},{40,32},{48,40},{56,48},{1,57}... | collective-permute-start | bytes 786440 | tf_op jit(solution)/shard_map/ppermute | solution.py:23
  38.8 45.5 %collective-permute-start.15 = (bf16[1736,512]{1,0:T(8,128)(2,1)}, bf16[1736,512]{1,0:T(8,128)(2,1)}, u32[]{:S(2)}, u32[]{:S(2)}) collective-permute-start(bf16[1736,512]{1,0:T(8,128)(2,1)} %shard_map.99.mine), channel_id=1, source_target_pairs={{0,1},{2,3},{5,4},{7,6},{8,9},{10,11},{13,12},{15,14},{16,17},{18,... | collective-permute-start | bytes 5333000 | tf_op jit(solution)/shard_map/ppermute | solution.py:459
  60.5 26.1 %collective-permute-start.14 = (f32[1024,256]{1,0:T(8,128)}, f32[1024,256]{1,0:T(8,128)}, u32[]{:S(2)}, u32[]{:S(2)}) collective-permute-start(f32[1024,256]{1,0:T(8,128)} %shard_map.98.pair_own), channel_id=1, source_target_pairs={{0,1},{1,0},{2,3},{3,2},{4,5},{5,4},{6,7},{7,6},{8,9},{9,8},{10,11... | collective-permute-start | bytes 3145736 | tf_op jit(solution)/shard_map/ppermute | solution.py:27
  75.4 19.1 %collective-permute-start.21 = (bf16[2,256,256]{2,1,0:T(8,128)(2,1)}, bf16[2,256,256]{2,1,0:T(8,128)(2,1)}, u32[]{:S(2)}, u32[]{:S(2)}) collective-permute-start(bf16[2,256,256]{2,1,0:T(8,128)(2,1)} %collective-permute-done.20.refs_7_), channel_id=1, source_target_pairs={{0,8},{8,16},{16,24},{24,32},{32,40},{40,48},{48,56},{56,0},{1,9},... | collective-permute-start | bytes 786440 | tf_op jit(solution)/shard_map/ppermute | solution.py:23
  81.2 16.0 %collective-permute-start.18 = (bf16[2,256,256]{2,1,0:T(8,128)(2,1)}, bf16[2,256,256]{2,1,0:T(8,128)(2,1)}, u32[]{:S(2)}, u32[]{:S(2)}) collective-permute-start(bf16[2,256,256]{2,1,0:T(8,128)(2,1)} %collective-permute-done.17.refs_2_), channel_id=1, source_target_pairs={{0,56},{8,0},{16,8},{24,16},{32,24},{40,32},{48,40},{56,48},{1,57}... | collective-permute-start | bytes 786440 | tf_op jit(solution)/shard_map/ppermute | solution.py:23
  94.5 11.7 %collective-permute-start.22 = (bf16[2,256,256]{2,1,0:T(8,128)(2,1)}, bf16[2,256,256]{2,1,0:T(8,128)(2,1)S(1)}, u32[]{:S(2)}, u32[]{:S(2)}) collective-permute-start(bf16[2,256,256]{2,1,0:T(8,128)(2,1)} %collective-permute-done.21.refs_6_), channel_id=1, source_target_pairs={{0,8},{8,16},{16,24},{24,32},{32,40},{40,48},{48,56},{56,0},{1,9},... | collective-permute-start | bytes 786440 | tf_op jit(solution)/shard_map/ppermute | solution.py:23
  97.2 13.8 %collective-permute-start.19 = (bf16[2,256,256]{2,1,0:T(8,128)(2,1)}, bf16[2,256,256]{2,1,0:T(8,128)(2,1)S(1)}, u32[]{:S(2)}, u32[]{:S(2)}) collective-permute-start(bf16[2,256,256]{2,1,0:T(8,128)(2,1)} %collective-permute-done.18.refs_3_), channel_id=1, source_target_pairs={{0,56},{8,0},{16,8},{24,16},{32,24},{40,32},{48,40},{56,48},{1,57}... | collective-permute-start | bytes 786440 | tf_op jit(solution)/shard_map/ppermute | solution.py:23
  97.2 16.3 %collective-permute-start.23 = (bf16[192,256]{1,0:T(8,128)(2,1)S(1)}, bf16[192,256]{1,0:T(8,128)(2,1)S(1)}, u32[]{:S(2)}, u32[]{:S(2)}) collective-permute-start(bf16[192,256]{1,0:T(8,128)(2,1)S(1)} %get-tuple-element.55), channel_id=1, source_target_pairs={{0,8},{8,16},{16,24},{24,32},{32,40},{40,48},{48,56},{56,0},{1,9},... | collective-permute-start | bytes 294920 | tf_op jit(solution)/shard_map/ppermute | solution.py:23
  98.7 14.8 %collective-permute-start.24 = (bf16[192,256]{1,0:T(8,128)(2,1)S(1)}, bf16[192,256]{1,0:T(8,128)(2,1)S(1)}, u32[]{:S(2)}, u32[]{:S(2)}) collective-permute-start(bf16[192,256]{1,0:T(8,128)(2,1)S(1)} %get-tuple-element.56), channel_id=1, source_target_pairs={{0,56},{8,0},{16,8},{24,16},{32,24},{40,32},{48,40},{56,48},{1,57}... | collective-permute-start | bytes 294920 | tf_op jit(solution)/shard_map/ppermute | solution.py:23
  129.8 11.7 %collective-permute-start.37 = (bf16[3584,256]{1,0:T(8,128)(2,1)S(1)}, bf16[3584,256]{1,0:T(8,128)(2,1)S(1)}, u32[]{:S(2)}, u32[]{:S(2)}) collective-permute-start(bf16[3584,256]{1,0:T(8,128)(2,1)S(1)} %shard_map.103.own), channel_id=1, source_target_pairs={{0,1},{1,0},{2,3},{3,2},{4,5},{5,4},{6,7},{7,6},{8,9},{9,8},{10,11... | collective-permute-start | bytes 5505032 | tf_op jit(solution)/shard_map/ppermute | solution.py:27
  151.4 28.9 %collective-permute-start.43 = (bf16[3,512,512]{2,1,0:T(8,128)(2,1)S(1)}, bf16[3,512,512]{2,1,0:T(8,128)(2,1)S(1)}, u32[]{:S(2)}, u32[]{:S(2)}) collective-permute-start(bf16[3,512,512]{2,1,0:T(8,128)(2,1)S(1)} %shard_map.104.updated.made), channel_id=1, source_target_pairs={{0,2},{2,0},{5,7},{7,5},{8,10},{10,8},{13,15},{15,13},{16,18},{18,... | collective-permute-start | bytes 4718600 | tf_op jit(solution)/shard_map/ppermute | solution.py:525
  152.2 28.2 %collective-permute-start.44 = (bf16[3,512,512]{2,1,0:T(8,128)(2,1)S(1)}, bf16[3,512,512]{2,1,0:T(8,128)(2,1)S(1)}, u32[]{:S(2)}, u32[]{:S(2)}) collective-permute-start(bf16[3,512,512]{2,1,0:T(8,128)(2,1)S(1)} %shard_map.104.updated.made), channel_id=1, source_target_pairs={{2,4},{0,6},{7,1},{5,3},{10,12},{8,14},{15,9},{13,11},{18,20},{16,... | collective-permute-start | bytes 4718600 | tf_op jit(solution)/shard_map/ppermute | solution.py:525
  159.3 20.4 %collective-permute-start.38 = (bf16[64,1024]{1,0:T(8,128)(2,1)S(1)}, bf16[64,1024]{1,0:T(8,128)(2,1)S(1)}, u32[]{:S(2)}, u32[]{:S(2)}) collective-permute-start(bf16[64,1024]{1,0:T(8,128)(2,1)S(1)} %get-tuple-element.62), channel_id=1, source_target_pairs={{0,2},{2,4},{4,6},{6,0},{1,3},{3,5},{5,7},{7,1},{8,10},{10,12},{12... | collective-permute-start | bytes 393224 | tf_op jit(solution)/shard_map/ppermute | solution.py:23
  159.6 20.2 %collective-permute-start.39 = (bf16[64,1024]{1,0:T(8,128)(2,1)S(1)}, bf16[64,1024]{1,0:T(8,128)(2,1)S(1)}, u32[]{:S(2)}, u32[]{:S(2)}) collective-permute-start(bf16[64,1024]{1,0:T(8,128)(2,1)S(1)} %get-tuple-element.63), channel_id=1, source_target_pairs={{0,6},{2,0},{4,2},{6,4},{1,7},{3,1},{5,3},{7,5},{8,14},{10,8},{12,... | collective-permute-start | bytes 393224 | tf_op jit(solution)/shard_map/ppermute | solution.py:23
  180.4 30.6 %collective-permute-start.45 = (bf16[3,256,512]{2,1,0:T(8,128)(2,1)S(1)}, bf16[3,256,512]{2,1,0:T(8,128)(2,1)S(1)}, u32[]{:S(2)}, u32[]{:S(2)}) collective-permute-start(bf16[3,256,512]{2,1,0:T(8,128)(2,1)S(1)} %slice.38), channel_id=1, source_target_pairs={{2,4},{0,6},{7,1},{5,3},{10,12},{8,14},{15,9},{13,11},{18,20},{16,... | collective-permute-start | bytes 2359304 | tf_op jit(solution)/shard_map/ppermute | solution.py:525
  181.8 29.2 %collective-permute-start.46 = (bf16[3,256,512]{2,1,0:T(8,128)(2,1)S(1)}, bf16[3,256,512]{2,1,0:T(8,128)(2,1)S(1)}, u32[]{:S(2)}, u32[]{:S(2)}) collective-permute-start(bf16[3,256,512]{2,1,0:T(8,128)(2,1)S(1)} %slice.39), channel_id=1, source_target_pairs={{1,3},{3,1},{4,6},{6,4},{9,11},{11,9},{12,14},{14,12},{17,19},{19,... | collective-permute-start | bytes 2359304 | tf_op jit(solution)/shard_map/ppermute | solution.py:525
  184.5 15.6 %collective-permute-start.40 = (bf16[128,1024]{1,0:T(8,128)(2,1)S(1)}, bf16[128,1024]{1,0:T(8,128)(2,1)S(1)}, u32[]{:S(2)}, u32[]{:S(2)}) collective-permute-start(bf16[128,1024]{1,0:T(8,128)(2,1)S(1)} %get-tuple-element.64), channel_id=1, source_target_pairs={{0,6},{2,0},{4,2},{6,4},{1,7},{3,1},{5,3},{7,5},{8,14},{10,8},{12,... | collective-permute-start | bytes 786440 | tf_op jit(solution)/shard_map/ppermute | solution.py:23
  185.9 14.2 %collective-permute-start.41 = (bf16[128,1024]{1,0:T(8,128)(2,1)S(1)}, bf16[128,1024]{1,0:T(8,128)(2,1)S(1)}, u32[]{:S(2)}, u32[]{:S(2)}) collective-permute-start(bf16[128,1024]{1,0:T(8,128)(2,1)S(1)} %get-tuple-element.65), channel_id=1, source_target_pairs={{0,2},{2,4},{4,6},{6,0},{1,3},{3,5},{5,7},{7,1},{8,10},{10,12},{12... | collective-permute-start | bytes 786440 | tf_op jit(solution)/shard_map/ppermute | solution.py:23
  (35 other events, 373.5 us)
where the time goes:
time: 214 us; the launch traced here: 213 us
  starting transfers between devices  83.4 us (39%)
  waiting for transfers between devices  74.6 us (35%)
  Pallas kernels  40.9 us (19%)
  local copies, waits for them, and re-layouts  6.74 us (3%)
  between operations  4.89 us (2%)
  other arithmetic  2.93 us (1%)
    ppermute x36, waiting for transfers between devices, moved(): lax.ppermute(value, axis, [(i, (i + steps) % count) for i in range(count)])  73 us
    ppermute x36, starting transfers between devices, moved(): lax.ppermute(value, axis, [(i, (i + steps) % count) for i in range(count)])  50.9 us
    pallas_call x13, Pallas kernels, kernel_call(): pl.pallas_call(body, out_shape=outs, in_specs=[pl.BlockSpec(memory_space=...  37.5 us
    ppermute x2, starting transfers between devices, swapped(): return lax.ppermute(value, 'head', [(0, 1), (1, 0)])  13.8 us
    ppermute x4, starting transfers between devices, to_head_chips(): got.append(lax.ppermute(part, ('y', 'head'), pairs))  11.4 us
    ppermute x4, starting transfers between devices, along(): lax.ppermute(value, ('y', 'head'), [(a * 2 + c, b * 2 + d) for a, c, b, d...  6.1 us
    unnamed x25, local copies, waits for them, and re-layouts  5.61 us
  transfers between devices with their start and end apart: 47, of which 15 were waited for; matrix products, arithmetic and copies ran while one was open for 1% of the time, Pallas kernels for 13%

commit v1 on v0

--- a/solution.py
+++ b/solution.py
@@ -57,15 +57,23 @@
     return pl.ds(pl.multiple_of(t * 256, 256), 256)
 
 
-def pack_body(place, w_ref, o_ref, extra_ref, *outs):
-    y = place[0]
+def pack_body(place, steps, w_hbm, o_hbm, *refs):
+    outs, (w_ref, o_ref, sems) = refs[:4], refs[4:]
+    fetches = [pltpu.make_async_copy(w_hbm, w_ref, sems.at[0]), pltpu.make_async_copy(o_hbm, o_ref, sems.at[1])]
+    for fetch in fetches:
+        fetch.start()
+    for fetch in fetches:
+        fetch.wait()
     for k, out in enumerate(outs):
-        j = lax.rem(y + k, 4)
+        j = lax.rem(place[0] + k, 4)
         columns = pl.ds(pl.multiple_of(j * 256, 256), 256)
         for row, component in enumerate((1, 2, 0)):
             out[row * 64 : row * 64 + 64, :] = w_ref[component, :, columns]
         out[192:256, :] = o_ref[:, columns]
-        out[256:264, :] = extra_ref[lax.div(j, 2)]
+        step = jnp.broadcast_to(steps[pl.ds(lax.div(j, 2), 1), :], (8, 128))
+        coarse = step.astype(bf16)
+        out[256:264, 0:128] = coarse
+        out[256:264, 128:256] = (step - coarse.astype(f32)).astype(bf16)
 
 
 def sort_body(place, a, b, c, d, key_value, query_out, steps):
@@ -202,7 +210,7 @@
     lax.fori_loop(0, 32, tile, 0)
 
 
-def newton_body(place, own, other, weights, rate, out, x_ref):
+def newton_body(place, own, other, weights, rate, top, bottom, x_ref):
     first = place[2] == 0
 
     def start(m, carry):
@@ -226,9 +234,9 @@
     def iteration(i, carry):
         m = lax.rem(i, 3)
         x = x_ref[m]
-        gram = dot(x, x, 0, 0).astype(bf16)
-        cubic = dot(x, gram, 1, 0)
-        quintic = dot(cubic.astype(bf16), gram, 1, 0)
+        gram = dot(x, x, 1, 1).astype(bf16)
+        cubic = dot(gram, x, 1, 0)
+        quintic = dot(gram, cubic.astype(bf16), 1, 0)
         x_ref[m] = (
             coef_linear * x.astype(f32) + coef_cubic * cubic + coef_quintic * quintic
         ).astype(bf16)
@@ -236,16 +244,19 @@
 
     lax.fori_loop(0, 3 * NS_ITERS, iteration, 0)
 
-    def update(i, carry):
-        m, span = lax.div(i, 8), spans(lax.rem(i, 8))
-        change = rate[0, 0] * x_ref[m, span, :].astype(f32)
-        out[m, span, :] = (weights[m, span, :].astype(f32) - change).astype(bf16)
-        return carry
-
-    lax.fori_loop(0, 24, update, 0)
-
-
-def apply_body(place, query_own, out_own, other, updated, out, top, bottom, *refs):
+    for first_tile, out in ((0, top), (4, bottom)):
+
+        def update(i, carry):
+            m, t = lax.div(i, 4), lax.rem(i, 4)
+            span = spans(t + first_tile)
+            change = rate[0, 0] * x_ref[m, span, :].astype(f32)
+            out[m, spans(t), :] = (weights[m, span, :].astype(f32) - change).astype(bf16)
+            return carry
+
+        lax.fori_loop(0, 12, update, 0)
+
+
+def apply_body(place, query_own, out_own, other, upper, lower, out, top, bottom, *refs):
     query, pre_ref, hidden, mixed, left_ref, right_ref, full = refs
     first = place[2] == 0
 
@@ -261,7 +272,10 @@
 
     def inner(i, carry):
         part = halves(lax.rem(i, 2))
-        pre_ref[lax.div(i, 2), part, :] = dot(query[part, :], updated[lax.div(i, 2)], 1, 0)
+        which = lax.div(i, 2)
+        pre_ref[which, part, :] = dot(query[part, 0:256], upper[which], 1, 0) + dot(
+            query[part, 256:512], lower[which], 1, 0
+        )
         return carry
 
     lax.fori_loop(0, 4, inner, 0)
@@ -274,7 +288,8 @@
     lax.fori_loop(0, 8, middle, 0)
 
     def outer(i, carry):
-        mixed[halves(i), :] = dot(hidden[halves(i), :], updated[2], 1, 1)
+        mixed[halves(i), 0:256] = dot(hidden[halves(i), :], upper[2], 1, 1)
+        mixed[halves(i), 256:512] = dot(hidden[halves(i), :], lower[2], 1, 1)
         return carry
 
     lax.fori_loop(0, 2, outer, 0)
@@ -349,17 +364,20 @@
         copy.wait()
 
 
-def emit_body(place, made, across, outward, out, sems):
+def emit_body(place, made_top, made_bottom, across_top, across_bottom, outward_top, outward_bottom, out, sems):
     slot = lax.rem(place[0], 2)
     owner = lax.div(place[0], 2) == place[2]
 
+    def head(top, bottom, which):
+        return [(top, out.at[which, :, pl.ds(0, 256)]), (bottom, out.at[which, :, pl.ds(256, 256)])]
+
     @pl.when(owner)
     def _():
-        copies([(made, out.at[slot]), (across, out.at[1 - slot])], sems)
+        copies(head(made_top, made_bottom, slot) + head(across_top, across_bottom, 1 - slot), sems)
 
     @pl.when(jnp.logical_not(owner))
     def _():
-        copies([(outward, out.at[1 - slot])], sems)
+        copies(head(outward_top, outward_bottom, 1 - slot), sems)
 
 
 def finish_body(place, relayed, traded, _, out, sems):
@@ -378,6 +396,16 @@
     for m in range(8):
         start = pl.multiple_of(lax.rem(place[1] + m, 8) * 256, 256)
         out[:, m * 256 : m * 256 + 256] = tokens[:, pl.ds(start, 256)]
+
+
+def join_body(place, *refs):
+    def tile(t, carry):
+        for i in range(4):
+            target = pl.ds(pl.multiple_of(t * 16 + i * 128, 16), 16)
+            refs[4][target, :] = refs[i][pl.ds(pl.multiple_of(t * 16, 16), 16), :]
+        return carry
+
+    lax.fori_loop(0, 8, tile, 0)
 
 
 def total_body(place, tokens, partial, low, high, out):
@@ -418,11 +446,21 @@
     core, y, z = lax.axis_index("head"), lax.axis_index("y"), lax.axis_index("z")
     place = jnp.stack([y, z, core])
 
-    steps = step_sizes[0].T
-    steps_high = lax.reduce_precision(steps, 8, 7)
-    extra = jnp.concatenate([steps_high, steps - steps_high], axis=1).astype(bf16)
-    extra = jnp.broadcast_to(extra[:, None, :], (2, 8, 256))
-    pieces = kernel_call(pack_body, [shape(264, 256)] * 4, [place, w_qkv[0], w_out[0].T, extra])
+    pieces = pl.pallas_call(
+        pack_body,
+        name="pack",
+        out_shape=[shape(264, 256)] * 4,
+        in_specs=[pl.BlockSpec(memory_space=pltpu.SMEM), pl.BlockSpec(memory_space=pltpu.VMEM)]
+        + [pl.BlockSpec(memory_space=pl.ANY)] * 2,
+        out_specs=[pl.BlockSpec(memory_space=pltpu.VMEM)] * 4,
+        scratch_shapes=[
+            pltpu.VMEM((3, 64, 1024), bf16),
+            pltpu.VMEM((64, 1024), bf16),
+            pltpu.SemaphoreType.DMA((2,)),
+        ],
+        compiler_params=pltpu.CompilerParams(vmem_limit_bytes=16 << 20),
+        cost_estimate=pl.CostEstimate(flops=0, bytes_accessed=1 << 20, transcendentals=0),
+    )(place, step_sizes[0].T, w_qkv[0], w_out[0].T)
     key_value, query_out, step_rows = kernel_call(
         sort_body,
         [shape(2, 256, 256), shape(2, 256, 256), shape(4, 8, 256, dtype=f32)],
@@ -439,8 +477,10 @@
 
     tokens, _ = lax.optimization_barrier((group_in[0], pieces[0]))
     turned = kernel_call(turn_body, shape(128, 2048), [place, tokens])
-    rows = jnp.concatenate(
-        [turned, moved(turned, "y", 1), moved(turned, "y", -1), moved(turned, "y", 2)]
+    rows = kernel_call(
+        join_body,
+        shape(512, 2048),
+        [place, turned] + [moved(turned, "y", hop) for hop in (1, -1, 2)],
     )
 
     part = lax.dynamic_slice(momentum[0], (y % 2, 0, z * 64, 0), (1, 3, 64, 512)).reshape(192, 512)
@@ -513,9 +553,9 @@
     )
 
     moment_other = swapped(moment_half)
-    made = kernel_call(
+    made_top, made_bottom = kernel_call(
         newton_body,
-        shape(3, 512, 512),
+        [shape(3, 256, 512)] * 2,
         [place, moment_half, moment_other, weights, rate],
         flops=2 * 512**3 * 18,
         scratch=[pltpu.VMEM((3, 512, 512), bf16)],
@@ -525,13 +565,18 @@
         return lax.ppermute(value, ("y", "head"), [(a * 2 + c, b * 2 + d) for a, c, b, d in hops])
 
     outer = [(1, 2), (0, 3), (3, 0), (2, 1)]
-    across = along(made, [(a, a // 2, a ^ 1, a // 2) for a in range(4)])
-    outward = along(made, [(a, a // 2, b, a // 2) for a, b in outer])
+
+    def first_hop(value):
+        across = along(value, [(a, a // 2, a ^ 1, a // 2) for a in range(4)])
+        return across, along(value, [(a, a // 2, b, a // 2) for a, b in outer])
+
+    across_top, outward_top = first_hop(made_top)
+    across_bottom, outward_bottom = first_hop(made_bottom)
 
     partial, top, bottom = kernel_call(
         apply_body,
         [shape(384, 1024, dtype=f32), shape(64, 1024), shape(64, 1024)],
-        [place, query_half, out_own, moment_other, made],
+        [place, query_half, out_own, moment_other, made_top, made_bottom],
         flops=2 * 512**3 * 5,
         scratch=[
             pltpu.VMEM((512, 512), bf16),
@@ -548,9 +593,8 @@
         [shape(128, 1024)] * 2,
         [place, partial, moved(top, "y", 1), moved(bottom, "y", -1)],
     )
-    across, outward, _ = lax.optimization_barrier((across, outward, low))
-    relayed = along(across[:, :256], [(a, a // 2, b, a // 2) for a, b in outer])
-    traded = along(outward[:, 256:], [(a, 1 - a // 2, a ^ 1, 1 - a // 2) for a in range(4)])
+    relayed = along(across_top, [(a, a // 2, b, a // 2) for a, b in outer])
+    traded = along(outward_bottom, [(a, 1 - a // 2, a ^ 1, 1 - a // 2) for a in range(4)])
 
     def emit(body, values, **more):
         count = len(values)
@@ -561,13 +605,15 @@
             + [pl.BlockSpec(memory_space=pltpu.VMEM)] * count
             + [pl.BlockSpec(memory_space=pl.ANY)] * (len(more) > 0),
             out_specs=pl.BlockSpec(memory_space=pl.ANY),
-            scratch_shapes=[pltpu.SemaphoreType.DMA((2,))],
+            scratch_shapes=[pltpu.SemaphoreType.DMA((4,))],
             compiler_params=pltpu.CompilerParams(vmem_limit_bytes=16 << 20),
             cost_estimate=pl.CostEstimate(flops=0, bytes_accessed=3 << 20, transcendentals=0),
             **({"input_output_aliases": {count + 1: 0}} if more else {}),
         )(place, *values, *more.values())
 
-    fast_next = emit(emit_body, (made, across, outward))
+    fast_next = emit(
+        emit_body, (made_top, made_bottom, across_top, across_bottom, outward_top, outward_bottom)
+    )
     fast_next = emit(finish_body, (relayed, traded), base=fast_next)
     sent_low, sent_high = moved(low, "y", -1), moved(high, "y", 1)
     layer_out = kernel_call(

time: 214 us -> 222 us (1.037)
  waiting for transfers between devices: 74.6 us -> 82.1 us
  other arithmetic: 2.93 us -> 0.32 us
  Pallas kernels: 40.9 us -> 43.5 us
    ppermute x36, waiting for transfers between devices: 73 us -> 79 us  [moved(): lax.ppermute(value, axis, [(i, (i + steps) % count) for i in range(count)])]
    ppermute x2, starting transfers between devices: 13.8 us -> 8.45 us  [swapped(): return lax.ppermute(value, 'head', [(0, 1), (1, 0)])]
    ppermute x36, starting transfers between devices: 50.9 us -> 54.6 us  [moved(): lax.ppermute(value, axis, [(i, (i + steps) % count) for i in range(count)])]
    ppermute x4 -> x6, starting transfers between devices: 6.1 us -> 7.74 us  [along(): lax.ppermute(value, ('y', 'head'), [(a * 2 + c, b * 2 + d) for a, c, b, d...]
    unnamed x25 -> x27, local copies, waits for them, and re-layouts: 5.61 us -> 6.41 us
  transfers between devices with their start and end apart: 47 -> 49, of which waited for: 15 -> 17; matrix products, arithmetic and copies ran while one was open for 1% -> 1% of each run, Pallas kernels for 13% -> 14%
where the time goes in v1:
time: 222 us
  starting transfers between devices  83.4 us (38%)
  waiting for transfers between devices  82.1 us (37%)
  Pallas kernels  43.5 us (20%)
  local copies, waits for them, and re-layouts  7.42 us (3%)
  between operations  4.89 us (2%)
    ppermute x36, waiting for transfers between devices, moved(): lax.ppermute(value, axis, [(i, (i + steps) % count) for i in range(count)])  79 us
    ppermute x36, starting transfers between devices, moved(): lax.ppermute(value, axis, [(i, (i + steps) % count) for i in range(count)])  54.6 us
    pallas_call x13, Pallas kernels, kernel_call(): pl.pallas_call(body, out_shape=outs, in_specs=[pl.BlockSpec(memory_space=...  39 us
    ppermute x4, starting transfers between devices, to_head_chips(): got.append(lax.ppermute(part, ('y', 'head'), pairs))  11.4 us
    ppermute x2, starting transfers between devices, swapped(): return lax.ppermute(value, 'head', [(0, 1), (1, 0)])  8.45 us
    ppermute x6, starting transfers between devices, along(): lax.ppermute(value, ('y', 'head'), [(a * 2 + c, b * 2 + d) for a, c, b, d...  7.74 us
    unnamed x27, local copies, waits for them, and re-layouts  6.41 us
  transfers between devices with their start and end apart: 49, of which 17 were waited for; matrix products, arithmetic and copies ran while one was open for 1% of the time, Pallas kernels for 14%

profile of v1, /device:TPU:1, one launch (start us, length us, event | category | flops | bytes accessed | tf_op | source)
XLA Modules:
  0.0 221.6 jit_solution(10420338360687457612)
XLA Ops:
  4.5 6.2 %collective-permute-start.3 = (bf16[264,256]{1,0:T(8,128)(2,1)S(1)}, bf16[264,256]{1,0:T(8,128)(2,1)S(1)}, u32[]{:S(2)}, u32[]{:S(2)}) collective-permute-start(bf16[264,256]{1,0:T(8,128)(2,1)S(1)} %get-tuple-element.35), channel_id=1, source_target_pairs={{0,0},{1,4},{2,1},{3,5},{4,2},{5,6},{6,3},{7,7},{8,8},{9,12},{10,9... | collective-permute-start | bytes 405512 | tf_op jit(solution)/shard_map/ppermute | solution.py:431
  25.1 4.0 %collective-permute-start.7 = (bf16[2,256,256]{2,1,0:T(8,128)(2,1)}, bf16[2,256,256]{2,1,0:T(8,128)(2,1)}, u32[]{:S(2)}, u32[]{:S(2)}) collective-permute-start(bf16[2,256,256]{2,1,0:T(8,128)(2,1)} %get-tuple-element.40.refs_0_), channel_id=1, source_target_pairs={{0,56},{8,0},{16,8},{24,16},{32,24},{40,32},{48,40},{56,48},{1,57}... | collective-permute-start | bytes 786440 | tf_op jit(solution)/shard_map/ppermute | solution.py:23
  29.1 4.9 %collective-permute-done.10.refs_7_ = bf16[2,256,256]{2,1,0:T(8,128)(2,1)} collective-permute-done((bf16[2,256,256]{2,1,0:T(8,128)(2,1)}, bf16[2,256,256]{2,1,0:T(8,128)(2,1)}, u32[]{:S(2)}, u32[]{:S(2)}) %collective-permute-start.10) | collective-permute-done | bytes 262176 | tf_op jit(solution)/shard_map/ppermute | solution.py:23
  39.5 3.9 %collective-permute-start.1 = (bf16[128,2048]{1,0:T(8,128)(2,1)}, bf16[128,2048]{1,0:T(8,128)(2,1)S(1)}, u32[]{:S(2)}, u32[]{:S(2)}) collective-permute-start(bf16[128,2048]{1,0:T(8,128)(2,1)} %shard_map.95.refs_0_), channel_id=1, source_target_pairs={{0,6},{2,0},{4,2},{6,4},{1,7},{3,1},{5,3},{7,5},{8,14},{10,8},{12,... | collective-permute-start | bytes 1572872 | tf_op jit(solution)/shard_map/ppermute | solution.py:23
  44.1 3.0 %collective-permute-start.8 = (bf16[2,256,256]{2,1,0:T(8,128)(2,1)}, bf16[2,256,256]{2,1,0:T(8,128)(2,1)S(1)}, u32[]{:S(2)}, u32[]{:S(2)}) collective-permute-start(bf16[2,256,256]{2,1,0:T(8,128)(2,1)} %collective-permute-done.7.refs_1_), channel_id=1, source_target_pairs={{0,56},{8,0},{16,8},{24,16},{32,24},{40,32},{48,40},{56,48},{1,57}... | collective-permute-start | bytes 786440 | tf_op jit(solution)/shard_map/ppermute | solution.py:23
  47.1 6.2 %collective-permute-done.8.refs_2_ = bf16[2,256,256]{2,1,0:T(8,128)(2,1)S(1)} collective-permute-done((bf16[2,256,256]{2,1,0:T(8,128)(2,1)}, bf16[2,256,256]{2,1,0:T(8,128)(2,1)S(1)}, u32[]{:S(2)}, u32[]{:S(2)}) %collective-permute-start.8) | collective-permute-done | bytes 262176 | tf_op jit(solution)/shard_map/ppermute | solution.py:23
  53.3 3.3 %collective-permute-start.9 = (bf16[2,256,256]{2,1,0:T(8,128)(2,1)S(1)}, bf16[2,256,256]{2,1,0:T(8,128)(2,1)S(1)}, u32[]{:S(2)}, u32[]{:S(2)}) collective-permute-start(bf16[2,256,256]{2,1,0:T(8,128)(2,1)S(1)} %collective-permute-done.8.refs_2_), channel_id=1, source_target_pairs={{0,56},{8,0},{16,8},{24,16},{32,24},{40,32},{48,40},{56,48},{1,57}... | collective-permute-start | bytes 786440 | tf_op jit(solution)/shard_map/ppermute | solution.py:23
  56.6 8.9 %collective-permute-done.1.refs_2_ = bf16[128,2048]{1,0:T(8,128)(2,1)S(1)} collective-permute-done((bf16[128,2048]{1,0:T(8,128)(2,1)}, bf16[128,2048]{1,0:T(8,128)(2,1)S(1)}, u32[]{:S(2)}, u32[]{:S(2)}) %collective-permute-start.1) | collective-permute-done | bytes 524320 | tf_op jit(solution)/shard_map/ppermute | solution.py:23
  66.9 4.9 %shard_map.98.pair_own = f32[1024,256]{1,0:T(8,128)} custom-call(s32[3]{0:T(128)S(1)} %pad_add_fusion.place, bf16[512,2048]{1,0:T(8,128)(2,1)S(1)} %shard_map.96.rows, bf16[2,256,256]{2,1,0:T(8,128)(2,1)} %get-tuple-element.40.refs_0_, bf16[2,256,256]{2,1,0:T(8,128)(2,1)} %collective-permute-done.7.refs_1_, ...), custom_call_target="tpu_custom_call" | custom-call | flops 1073741824 | bytes 4194304 | tf_op jit(solution)/shard_map/pallas_call | solution.py:36
  71.8 3.0 %collective-permute-start.16 = (bf16[2,256,256]{2,1,0:T(8,128)(2,1)S(1)}, bf16[2,256,256]{2,1,0:T(8,128)(2,1)}, u32[]{:S(2)}, u32[]{:S(2)}) collective-permute-start(bf16[2,256,256]{2,1,0:T(8,128)(2,1)S(1)} %get-tuple-element.47.refs_0_), channel_id=1, source_target_pairs={{0,56},{8,0},{16,8},{24,16},{32,24},{40,32},{48,40},{56,48},{1,57}... | collective-permute-start | bytes 786440 | tf_op jit(solution)/shard_map/ppermute | solution.py:23
  74.8 5.2 %collective-permute-done.16.refs_1_ = bf16[2,256,256]{2,1,0:T(8,128)(2,1)} collective-permute-done((bf16[2,256,256]{2,1,0:T(8,128)(2,1)S(1)}, bf16[2,256,256]{2,1,0:T(8,128)(2,1)}, u32[]{:S(2)}, u32[]{:S(2)}) %collective-permute-start.16) | collective-permute-done | bytes 262176 | tf_op jit(solution)/shard_map/ppermute | solution.py:23
  80.0 3.5 %collective-permute-start.17 = (bf16[2,256,256]{2,1,0:T(8,128)(2,1)}, bf16[2,256,256]{2,1,0:T(8,128)(2,1)}, u32[]{:S(2)}, u32[]{:S(2)}) collective-permute-start(bf16[2,256,256]{2,1,0:T(8,128)(2,1)} %collective-permute-done.16.refs_1_), channel_id=1, source_target_pairs={{0,56},{8,0},{16,8},{24,16},{32,24},{40,32},{48,40},{56,48},{1,57}... | collective-permute-start | bytes 786440 | tf_op jit(solution)/shard_map/ppermute | solution.py:23
  83.6 4.6 %collective-permute-done.17.refs_2_ = bf16[2,256,256]{2,1,0:T(8,128)(2,1)} collective-permute-done((bf16[2,256,256]{2,1,0:T(8,128)(2,1)}, bf16[2,256,256]{2,1,0:T(8,128)(2,1)}, u32[]{:S(2)}, u32[]{:S(2)}) %collective-permute-start.17) | collective-permute-done | bytes 262176 | tf_op jit(solution)/shard_map/ppermute | solution.py:23
  88.2 3.4 %collective-permute-start.18 = (bf16[2,256,256]{2,1,0:T(8,128)(2,1)}, bf16[2,256,256]{2,1,0:T(8,128)(2,1)}, u32[]{:S(2)}, u32[]{:S(2)}) collective-permute-start(bf16[2,256,256]{2,1,0:T(8,128)(2,1)} %collective-permute-done.17.refs_2_), channel_id=1, source_target_pairs={{0,56},{8,0},{16,8},{24,16},{32,24},{40,32},{48,40},{56,48},{1,57}... | collective-permute-start | bytes 786440 | tf_op jit(solution)/shard_map/ppermute | solution.py:23
  94.1 5.2 %shard_map.101 = (f32[192,256]{1,0:T(8,128)S(1)}, bf16[192,256]{1,0:T(8,128)(2,1)S(1)}, bf16[192,256]{1,0:T(8,128)(2,1)S(1)}, bf16[192,256]{1,0:T(8,128)(2,1)S(1...) custom-call(s32[3]{0:T(128)S(1)} %pad_add_fusion.place, ...), custom_call_target="tpu_custom_call" | custom-call | flops 805306368 | bytes 3672064 | tf_op jit(solution)/shard_map/pallas_call | solution.py:36
  104.9 4.5 %collective-permute-done.26 = bf16[192,256]{1,0:T(8,128)(2,1)S(1)} collective-permute-done((bf16[192,256]{1,0:T(8,128)(2,1)S(1)}, bf16[192,256]{1,0:T(8,128)(2,1)S(1)}, u32[]{:S(2)}, u32[]{:S(2)}) %collective-permute-start.26) | collective-permute-done | bytes 98336 | tf_op jit(solution)/shard_map/ppermute | solution.py:23
  130.4 3.4 %collective-permute-done.33.refs_4_ = bf16[192,256]{1,0:T(8,128)(2,1)S(1)} collective-permute-done((bf16[192,256]{1,0:T(8,128)(2,1)S(1)}, bf16[192,256]{1,0:T(8,128)(2,1)S(1)}, u32[]{:S(2)}, u32[]{:S(2)}) %collective-permute-start.33) | collective-permute-done | bytes 98336 | tf_op jit(solution)/shard_map/ppermute | solution.py:23
  136.5 8.4 %collective-permute-start.37 = (bf16[3584,256]{1,0:T(8,128)(2,1)S(1)}, bf16[3584,256]{1,0:T(8,128)(2,1)S(1)}, u32[]{:S(2)}, u32[]{:S(2)}) collective-permute-start(bf16[3584,256]{1,0:T(8,128)(2,1)S(1)} %shard_map.103.own), channel_id=1, source_target_pairs={{0,1},{1,0},{2,3},{3,2},{4,5},{5,4},{6,7},{7,6},{8,9},{9,8},{10,11... | collective-permute-start | bytes 5505032 | tf_op jit(solution)/shard_map/ppermute | solution.py:27
  148.4 10.0 %shard_map.104 = (bf16[3,256,512]{2,1,0:T(8,128)(2,1)S(1)}, bf16[3,256,512]{2,1,0:T(8,128)(2,1)S(1)}) custom-call(s32[3]{0:T(128)S(1)} %pad_add_fusion.place, bf16[3584,256]{1,0:T(8,128)(2,1)S(1)} %shard_map.103.own, bf16[3584,256]{1,0:T(8,128)(2,1)S(1)} %collective-permute-done.37.other, bf16[3,512,512]{2,1,0:T(8,128)(2,1)S(1)} %get-tuple-element.44.weights, ...), custom_call_target="tpu_custom_call" | custom-call | flops 4831838208 | bytes 5242884 | tf_op jit(solution)/shard_map/pallas_call | solution.py:36
  160.5 5.7 %shard_map.105 = (f32[384,1024]{1,0:T(8,128)S(1)}, bf16[64,1024]{1,0:T(8,128)(2,1)S(1)}, bf16[64,1024]{1,0:T(8,128)(2,1)S(1)}) custom-call(s32[3]{0:T(128)S(1)} %pad_add_fusion.place, f32[512,256]{1,0:T(8,128)S(1)} %get-tuple-element.48.query_own, bf16[1024,256]{1,0:T(8,128)(2,1)S(1)} %get-tuple-element.49.out_own, ...), custom_call_target="tpu_custom_call" | custom-call | flops 1342177280 | bytes 4456448 | tf_op jit(solution)/shard_map/pallas_call | solution.py:36
  167.9 3.0 %collective-permute-start.39 = (bf16[64,1024]{1,0:T(8,128)(2,1)S(1)}, bf16[64,1024]{1,0:T(8,128)(2,1)S(1)}, u32[]{:S(2)}, u32[]{:S(2)}) collective-permute-start(bf16[64,1024]{1,0:T(8,128)(2,1)S(1)} %get-tuple-element.65), channel_id=1, source_target_pairs={{0,6},{2,0},{4,2},{6,4},{1,7},{3,1},{5,3},{7,5},{8,14},{10,8},{12,... | collective-permute-start | bytes 393224 | tf_op jit(solution)/shard_map/ppermute | solution.py:23
  170.9 5.8 %collective-permute-done.38.top = bf16[64,1024]{1,0:T(8,128)(2,1)S(1)} collective-permute-done((bf16[64,1024]{1,0:T(8,128)(2,1)S(1)}, bf16[64,1024]{1,0:T(8,128)(2,1)S(1)}, u32[]{:S(2)}, u32[]{:S(2)}) %collective-permute-start.38) | collective-permute-done | bytes 131104 | tf_op jit(solution)/shard_map/ppermute | solution.py:23
  186.5 20.7 %collective-permute-done.41.high = bf16[128,1024]{1,0:T(8,128)(2,1)S(1)} collective-permute-done((bf16[128,1024]{1,0:T(8,128)(2,1)S(1)}, bf16[128,1024]{1,0:T(8,128)(2,1)S(1)}, u32[]{:S(2)}, u32[]{:S(2)}) %collective-permute-start.41) | collective-permute-done | bytes 262176 | tf_op jit(solution)/shard_map/ppermute | solution.py:23
  209.0 8.4 %collective-permute-done.42 = bf16[1,128,1024]{2,1,0:T(8,128)(2,1)S(1)} collective-permute-done((bf16[1,128,1024]{2,1,0:T(8,128)(2,1)S(1)}, bf16[1,128,1024]{2,1,0:T(8,128)(2,1)S(1)}, u32[]{:S(2)}, u32[]{:S(2)}) %collective-permute-start.42) | collective-permute-done | bytes 262176 | tf_op jit(solution)/shard_map/ppermute | solution.py:23
  (132 shorter events, 76.5 us)
Async XLA Ops:
  4.5 15.9 %collective-permute-start.3 = (bf16[264,256]{1,0:T(8,128)(2,1)S(1)}, bf16[264,256]{1,0:T(8,128)(2,1)S(1)}, u32[]{:S(2)}, u32[]{:S(2)}) collective-permute-start(bf16[264,256]{1,0:T(8,128)(2,1)S(1)} %get-tuple-element.35), channel_id=1, source_target_pairs={{0,0},{1,4},{2,1},{3,5},{4,2},{5,6},{6,3},{7,7},{8,8},{9,12},{10,9... | collective-permute-start | bytes 405512 | tf_op jit(solution)/shard_map/ppermute | solution.py:431
  18.3 25.8 %collective-permute-start = (bf16[128,2048]{1,0:T(8,128)(2,1)}, bf16[128,2048]{1,0:T(8,128)(2,1)}, u32[]{:S(2)}, u32[]{:S(2)}) collective-permute-start(bf16[128,2048]{1,0:T(8,128)(2,1)} %shard_map.95.refs_0_), channel_id=1, source_target_pairs={{0,2},{2,4},{4,6},{6,0},{1,3},{3,5},{5,7},{7,1},{8,10},{10,12},{12... | collective-permute-start | bytes 1572872 | tf_op jit(solution)/shard_map/ppermute | solution.py:23
  23.2 10.8 %collective-permute-start.10 = (bf16[2,256,256]{2,1,0:T(8,128)(2,1)}, bf16[2,256,256]{2,1,0:T(8,128)(2,1)}, u32[]{:S(2)}, u32[]{:S(2)}) collective-permute-start(bf16[2,256,256]{2,1,0:T(8,128)(2,1)} %get-tuple-element.40.refs_0_), channel_id=1, source_target_pairs={{0,8},{8,16},{16,24},{24,32},{32,40},{40,48},{48,56},{56,0},{1,9},... | collective-permute-start | bytes 786440 | tf_op jit(solution)/shard_map/ppermute | solution.py:23
  25.1 18.3 %collective-permute-start.7 = (bf16[2,256,256]{2,1,0:T(8,128)(2,1)}, bf16[2,256,256]{2,1,0:T(8,128)(2,1)}, u32[]{:S(2)}, u32[]{:S(2)}) collective-permute-start(bf16[2,256,256]{2,1,0:T(8,128)(2,1)} %get-tuple-element.40.refs_0_), channel_id=1, source_target_pairs={{0,56},{8,0},{16,8},{24,16},{32,24},{40,32},{48,40},{56,48},{1,57}... | collective-permute-start | bytes 786440 | tf_op jit(solution)/shard_map/ppermute | solution.py:23
  34.1 13.0 %collective-permute-start.11 = (bf16[2,256,256]{2,1,0:T(8,128)(2,1)}, bf16[2,256,256]{2,1,0:T(8,128)(2,1)}, u32[]{:S(2)}, u32[]{:S(2)}) collective-permute-start(bf16[2,256,256]{2,1,0:T(8,128)(2,1)} %collective-permute-done.10.refs_7_), channel_id=1, source_target_pairs={{0,8},{8,16},{16,24},{24,32},{32,40},{40,48},{48,56},{56,0},{1,9},... | collective-permute-start | bytes 786440 | tf_op jit(solution)/shard_map/ppermute | solution.py:23
  38.2 53.5 %collective-permute-start.15 = (bf16[1736,512]{1,0:T(8,128)(2,1)}, bf16[1736,512]{1,0:T(8,128)(2,1)}, u32[]{:S(2)}, u32[]{:S(2)}) collective-permute-start(bf16[1736,512]{1,0:T(8,128)(2,1)} %shard_map.99.mine), channel_id=1, source_target_pairs={{0,1},{2,3},{5,4},{7,6},{8,9},{10,11},{13,12},{15,14},{16,17},{18,... | collective-permute-start | bytes 5333000 | tf_op jit(solution)/shard_map/ppermute | solution.py:499
  39.5 25.9 %collective-permute-start.1 = (bf16[128,2048]{1,0:T(8,128)(2,1)}, bf16[128,2048]{1,0:T(8,128)(2,1)S(1)}, u32[]{:S(2)}, u32[]{:S(2)}) collective-permute-start(bf16[128,2048]{1,0:T(8,128)(2,1)} %shard_map.95.refs_0_), channel_id=1, source_target_pairs={{0,6},{2,0},{4,2},{6,4},{1,7},{3,1},{5,3},{7,5},{8,14},{10,8},{12,... | collective-permute-start | bytes 1572872 | tf_op jit(solution)/shard_map/ppermute | solution.py:23
  43.4 22.0 %collective-permute-start.2 = (bf16[128,2048]{1,0:T(8,128)(2,1)}, bf16[128,2048]{1,0:T(8,128)(2,1)S(1)}, u32[]{:S(2)}, u32[]{:S(2)}) collective-permute-start(bf16[128,2048]{1,0:T(8,128)(2,1)} %shard_map.95.refs_0_), channel_id=1, source_target_pairs={{0,4},{2,6},{4,0},{6,2},{1,5},{3,7},{5,1},{7,3},{8,12},{10,14},{12... | collective-permute-start | bytes 1572872 | tf_op jit(solution)/shard_map/ppermute | solution.py:23
  53.3 13.6 %collective-permute-start.9 = (bf16[2,256,256]{2,1,0:T(8,128)(2,1)S(1)}, bf16[2,256,256]{2,1,0:T(8,128)(2,1)S(1)}, u32[]{:S(2)}, u32[]{:S(2)}) collective-permute-start(bf16[2,256,256]{2,1,0:T(8,128)(2,1)S(1)} %collective-permute-done.8.refs_2_), channel_id=1, source_target_pairs={{0,56},{8,0},{16,8},{24,16},{32,24},{40,32},{48,40},{56,48},{1,57}... | collective-permute-start | bytes 786440 | tf_op jit(solution)/shard_map/ppermute | solution.py:23
  71.8 22.3 %collective-permute-start.14 = (f32[1024,256]{1,0:T(8,128)}, f32[1024,256]{1,0:T(8,128)}, u32[]{:S(2)}, u32[]{:S(2)}) collective-permute-start(f32[1024,256]{1,0:T(8,128)} %shard_map.98.pair_own), channel_id=1, source_target_pairs={{0,1},{1,0},{2,3},{3,2},{4,5},{5,4},{6,7},{7,6},{8,9},{9,8},{10,11... | collective-permute-start | bytes 3145736 | tf_op jit(solution)/shard_map/ppermute | solution.py:27
  83.5 15.9 %collective-permute-start.21 = (bf16[2,256,256]{2,1,0:T(8,128)(2,1)}, bf16[2,256,256]{2,1,0:T(8,128)(2,1)}, u32[]{:S(2)}, u32[]{:S(2)}) collective-permute-start(bf16[2,256,256]{2,1,0:T(8,128)(2,1)} %collective-permute-done.20.refs_7_), channel_id=1, source_target_pairs={{0,8},{8,16},{16,24},{24,32},{32,40},{40,48},{48,56},{56,0},{1,9},... | collective-permute-start | bytes 786440 | tf_op jit(solution)/shard_map/ppermute | solution.py:23
  88.2 12.7 %collective-permute-start.18 = (bf16[2,256,256]{2,1,0:T(8,128)(2,1)}, bf16[2,256,256]{2,1,0:T(8,128)(2,1)}, u32[]{:S(2)}, u32[]{:S(2)}) collective-permute-start(bf16[2,256,256]{2,1,0:T(8,128)(2,1)} %collective-permute-done.17.refs_2_), channel_id=1, source_target_pairs={{0,56},{8,0},{16,8},{24,16},{32,24},{40,32},{48,40},{56,48},{1,57}... | collective-permute-start | bytes 786440 | tf_op jit(solution)/shard_map/ppermute | solution.py:23
  99.4 14.6 %collective-permute-start.22 = (bf16[2,256,256]{2,1,0:T(8,128)(2,1)}, bf16[2,256,256]{2,1,0:T(8,128)(2,1)S(1)}, u32[]{:S(2)}, u32[]{:S(2)}) collective-permute-start(bf16[2,256,256]{2,1,0:T(8,128)(2,1)} %collective-permute-done.21.refs_6_), channel_id=1, source_target_pairs={{0,8},{8,16},{16,24},{24,32},{32,40},{40,48},{48,56},{56,0},{1,9},... | collective-permute-start | bytes 786440 | tf_op jit(solution)/shard_map/ppermute | solution.py:23
  100.9 16.8 %collective-permute-start.19 = (bf16[2,256,256]{2,1,0:T(8,128)(2,1)}, bf16[2,256,256]{2,1,0:T(8,128)(2,1)S(1)}, u32[]{:S(2)}, u32[]{:S(2)}) collective-permute-start(bf16[2,256,256]{2,1,0:T(8,128)(2,1)} %collective-permute-done.18.refs_3_), channel_id=1, source_target_pairs={{0,56},{8,0},{16,8},{24,16},{32,24},{40,32},{48,40},{56,48},{1,57}... | collective-permute-start | bytes 786440 | tf_op jit(solution)/shard_map/ppermute | solution.py:23
  104.6 15.6 %collective-permute-start.24 = (bf16[192,256]{1,0:T(8,128)(2,1)S(1)}, bf16[192,256]{1,0:T(8,128)(2,1)S(1)}, u32[]{:S(2)}, u32[]{:S(2)}) collective-permute-start(bf16[192,256]{1,0:T(8,128)(2,1)S(1)} %get-tuple-element.56), channel_id=1, source_target_pairs={{0,56},{8,0},{16,8},{24,16},{32,24},{40,32},{48,40},{56,48},{1,57}... | collective-permute-start | bytes 294920 | tf_op jit(solution)/shard_map/ppermute | solution.py:23
  109.4 10.8 %collective-permute-start.23 = (bf16[192,256]{1,0:T(8,128)(2,1)S(1)}, bf16[192,256]{1,0:T(8,128)(2,1)S(1)}, u32[]{:S(2)}, u32[]{:S(2)}) collective-permute-start(bf16[192,256]{1,0:T(8,128)(2,1)S(1)} %get-tuple-element.55), channel_id=1, source_target_pairs={{0,8},{8,16},{16,24},{24,32},{32,40},{40,48},{48,56},{56,0},{1,9},... | collective-permute-start | bytes 294920 | tf_op jit(solution)/shard_map/ppermute | solution.py:23
  136.5 11.9 %collective-permute-start.37 = (bf16[3584,256]{1,0:T(8,128)(2,1)S(1)}, bf16[3584,256]{1,0:T(8,128)(2,1)S(1)}, u32[]{:S(2)}, u32[]{:S(2)}) collective-permute-start(bf16[3584,256]{1,0:T(8,128)(2,1)S(1)} %shard_map.103.own), channel_id=1, source_target_pairs={{0,1},{1,0},{2,3},{3,2},{4,5},{5,4},{6,7},{7,6},{8,9},{9,8},{10,11... | collective-permute-start | bytes 5505032 | tf_op jit(solution)/shard_map/ppermute | solution.py:27
  158.4 21.9 %collective-permute-start.43 = (bf16[3,256,512]{2,1,0:T(8,128)(2,1)S(1)}, bf16[3,256,512]{2,1,0:T(8,128)(2,1)S(1)}, u32[]{:S(2)}, u32[]{:S(2)}) collective-permute-start(bf16[3,256,512]{2,1,0:T(8,128)(2,1)S(1)} %get-tuple-element.61.upper.made_top), channel_id=1, source_target_pairs={{0,2},{2,0},{5,7},{7,5},{8,10},{10,8},{13,15},{15,13},{16,18},{18,... | collective-permute-start | bytes 2359304 | tf_op jit(solution)/shard_map/ppermute | solution.py:565
  159.2 22.5 %collective-permute-start.45 = (bf16[3,256,512]{2,1,0:T(8,128)(2,1)S(1)}, bf16[3,256,512]{2,1,0:T(8,128)(2,1)S(1)}, u32[]{:S(2)}, u32[]{:S(2)}) collective-permute-start(bf16[3,256,512]{2,1,0:T(8,128)(2,1)S(1)} %get-tuple-element.62.lower.made_bottom), channel_id=1, source_target_pairs={{2,4},{0,6},{7,1},{5,3},{10,12},{8,14},{15,9},{13,11},{18,20},{16,... | collective-permute-start | bytes 2359304 | tf_op jit(solution)/shard_map/ppermute | solution.py:565
  178.3 39.1 %collective-permute-start.47 = (bf16[3,256,512]{2,1,0:T(8,128)(2,1)S(1)}, bf16[3,256,512]{2,1,0:T(8,128)(2,1)S(1)}, u32[]{:S(2)}, u32[]{:S(2)}) collective-permute-start(bf16[3,256,512]{2,1,0:T(8,128)(2,1)S(1)} %get-tuple-element.62.lower.made_bottom), channel_id=1, source_target_pairs={{0,2},{2,0},{5,7},{7,5},{8,10},{10,8},{13,15},{15,13},{16,18},{18,... | collective-permute-start | bytes 2359304 | tf_op jit(solution)/shard_map/ppermute | solution.py:565
  179.0 38.4 %collective-permute-start.48 = (bf16[3,256,512]{2,1,0:T(8,128)(2,1)S(1)}, bf16[3,256,512]{2,1,0:T(8,128)(2,1)S(1)}, u32[]{:S(2)}, u32[]{:S(2)}) collective-permute-start(bf16[3,256,512]{2,1,0:T(8,128)(2,1)S(1)} %get-tuple-element.61.upper.made_top), channel_id=1, source_target_pairs={{2,4},{0,6},{7,1},{5,3},{10,12},{8,14},{15,9},{13,11},{18,20},{16,... | collective-permute-start | bytes 2359304 | tf_op jit(solution)/shard_map/ppermute | solution.py:565
  180.3 38.8 %collective-permute-start.44 = (bf16[3,256,512]{2,1,0:T(8,128)(2,1)S(1)}, bf16[3,256,512]{2,1,0:T(8,128)(2,1)S(1)}, u32[]{:S(2)}, u32[]{:S(2)}) collective-permute-start(bf16[3,256,512]{2,1,0:T(8,128)(2,1)S(1)} %collective-permute-done.43.across_top), channel_id=1, source_target_pairs={{2,4},{0,6},{7,1},{5,3},{10,12},{8,14},{15,9},{13,11},{18,20},{16,... | collective-permute-start | bytes 2359304 | tf_op jit(solution)/shard_map/ppermute | solution.py:565
  181.6 37.5 %collective-permute-start.46 = (bf16[3,256,512]{2,1,0:T(8,128)(2,1)S(1)}, bf16[3,256,512]{2,1,0:T(8,128)(2,1)S(1)}, u32[]{:S(2)}, u32[]{:S(2)}) collective-permute-start(bf16[3,256,512]{2,1,0:T(8,128)(2,1)S(1)} %collective-permute-done.45.outward_bottom), channel_id=1, source_target_pairs={{1,3},{3,1},{4,6},{6,4},{9,11},{11,9},{12,14},{14,12},{17,19},{19,... | collective-permute-start | bytes 2359304 | tf_op jit(solution)/shard_map/ppermute | solution.py:565
  184.2 23.1 %collective-permute-start.41 = (bf16[128,1024]{1,0:T(8,128)(2,1)S(1)}, bf16[128,1024]{1,0:T(8,128)(2,1)S(1)}, u32[]{:S(2)}, u32[]{:S(2)}) collective-permute-start(bf16[128,1024]{1,0:T(8,128)(2,1)S(1)} %get-tuple-element.67), channel_id=1, source_target_pairs={{0,2},{2,4},{4,6},{6,0},{1,3},{3,5},{5,7},{7,1},{8,10},{10,12},{12... | collective-permute-start | bytes 786440 | tf_op jit(solution)/shard_map/ppermute | solution.py:23
  (38 other events, 426.7 us)

commit v2 on v1

--- a/solution.py
+++ b/solution.py
@@ -76,7 +76,7 @@
         out[256:264, 128:256] = (step - coarse.astype(f32)).astype(bf16)
 
 
-def sort_body(place, a, b, c, d, key_value, query_out, steps):
+def sort_body(place, a, b, c, d, key_value, query_out, step):
     slot = 2 * lax.rem(place[0], 2) + place[2]
     for k, piece in enumerate((a, b, c, d)):
         source = lax.rem(slot + 4 - k, 4)
@@ -84,7 +84,10 @@
         for i in range(2):
             key_value[i, rows, :] = piece[i * 64 : i * 64 + 64, :]
             query_out[i, rows, :] = piece[i * 64 + 128 : i * 64 + 192, :]
-        steps[source] = piece[256:264, :].astype(f32)
+        terms = piece[256:264, :].astype(f32)
+        column = jnp.broadcast_to(terms[0:1, 0:128] + terms[0:1, 128:256], (128, 128)).T
+        block = lax.rem(source + 4 - place[0], 4)
+        step[pl.ds(pl.multiple_of(block * 128, 128), 128), :] = column
 
 
 def project_body(place, rows, *refs):
@@ -160,7 +163,7 @@
         low, high = normed(pair_own[span, :], pair_other[span, :], first, 1e-06)
         left[0, span, 0:256] = low
         left[0, span, 256:512] = high
-        scale = step[span, :]
+        scale = step[span, 0:1]
         low, high = sides(pair_own[down, :], pair_other[down, :], first)
         left[1, span, 0:256] = (-(scale * low.astype(bf16).astype(f32))).astype(bf16)
         left[1, span, 256:512] = (-(scale * high.astype(bf16).astype(f32))).astype(bf16)
@@ -210,7 +213,7 @@
     lax.fori_loop(0, 32, tile, 0)
 
 
-def newton_body(place, own, other, weights, rate, top, bottom, x_ref):
+def newton_body(place, own, other, weights, terms, top, bottom, x_ref):
     first = place[2] == 0
 
     def start(m, carry):
@@ -244,12 +247,13 @@
 
     lax.fori_loop(0, 3 * NS_ITERS, iteration, 0)
 
+    rate = terms[1:2, 0:1] + terms[3:4, 0:1] + terms[5:6, 0:1]
     for first_tile, out in ((0, top), (4, bottom)):
 
         def update(i, carry):
             m, t = lax.div(i, 4), lax.rem(i, 4)
             span = spans(t + first_tile)
-            change = rate[0, 0] * x_ref[m, span, :].astype(f32)
+            change = rate * x_ref[m, span, :].astype(f32)
             out[m, spans(t), :] = (weights[m, span, :].astype(f32) - change).astype(bf16)
             return carry
 
@@ -309,29 +313,57 @@
             right_ref[...], other[halves(i + 10), :], 1, 1
         )
         columns = halves(i)
-        out[:, columns] = full[i, 0:384, :]
-        top[:, columns] = full[i, 384:448, :].astype(bf16)
-        bottom[:, columns] = full[i, 448:512, :].astype(bf16)
+        out[0:256, columns] = full[i, 0:256, :]
+        out[256:384, columns] = full[i, 384:512, :]
+        top[:, columns] = full[i, 256:320, :].astype(bf16)
+        bottom[:, columns] = full[i, 320:384, :].astype(bf16)
         return carry
 
     lax.fori_loop(0, 4, last, 0)
 
 
 def relay_body(place, partial, top, bottom, low_out, high_out):
-    low_out[0:64, :] = partial[128:192, :].astype(bf16)
-    low_out[64:128, :] = (partial[192:256, :] + bottom[...].astype(f32)).astype(bf16)
-    high_out[0:64, :] = (partial[256:320, :] + top[...].astype(f32)).astype(bf16)
-    high_out[64:128, :] = partial[320:384, :].astype(bf16)
-
-
-def payload_body(place, weights, momentum, scalars, out):
-    def tile(i, carry):
-        out[spans(i), :] = weights[lax.rem(place[0], 2), lax.div(i, 8), spans(lax.rem(i, 8)), :]
-        return carry
-
-    lax.fori_loop(0, 24, tile, 0)
-    out[1536:1728, :] = momentum[...]
-    out[1728:1736, :] = scalars[...]
+    high_out[0:64, :] = (partial[128:192, :] + top[...].astype(f32)).astype(bf16)
+    high_out[64:128, :] = partial[192:256, :].astype(bf16)
+    low_out[0:64, :] = partial[256:320, :].astype(bf16)
+    low_out[64:128, :] = (partial[320:384, :] + bottom[...].astype(f32)).astype(bf16)
+
+
+def payload_body(place, decays, rates, weights, momentum, out, part, sems):
+    slot = lax.rem(place[0], 2)
+    rows = pl.ds(pl.multiple_of(place[1] * 64, 64), 64)
+    fetches = [pltpu.make_async_copy(momentum.at[slot, :, rows], part, sems.at[3])]
+    for m in range(3):
+        target = out.at[pl.ds(m * 512, 512)]
+        fetches.append(pltpu.make_async_copy(weights.at[slot, m], target, sems.at[m]))
+    for fetch in fetches:
+        fetch.start()
+    terms = jnp.zeros((8, 512), f32)
+    which = lax.broadcasted_iota(jnp.int32, (8, 512), 0)
+    for i, scalars in enumerate((decays, rates)):
+        value = jnp.full((8, 512), scalars[slot])
+        for k in range(3):
+            term = value.astype(bf16).astype(f32)
+            terms = jnp.where(which == 2 * k + i, term, terms)
+            value = value - term
+    out[1728:1736, :] = terms.astype(bf16)
+    for fetch in fetches:
+        fetch.wait()
+    for m in range(3):
+        out[1536 + m * 64 : 1600 + m * 64, :] = part[m]
+
+
+def sum_body(place, *refs):
+    total = refs[0][...].astype(f32)
+    for ref in refs[1:-1]:
+        total = total + ref[...].astype(f32)
+    refs[-1][...] = total.astype(bf16)
+
+
+def moment_body(place, own, momentum, terms, a, b, c, d, out):
+    decay = terms[0:1, 0:1] + terms[2:3, 0:1] + terms[4:5, 0:1]
+    total = own[...] + a[...].astype(f32) + b[...].astype(f32) + c[...].astype(f32) + d[...].astype(f32)
+    out[...] = (decay * momentum[...] + total).astype(bf16)
 
 
 def choose_body(place, mine, arrived, weights_out, momentum_out, scalars_out):
@@ -451,7 +483,7 @@
         name="pack",
         out_shape=[shape(264, 256)] * 4,
         in_specs=[pl.BlockSpec(memory_space=pltpu.SMEM), pl.BlockSpec(memory_space=pltpu.VMEM)]
-        + [pl.BlockSpec(memory_space=pl.ANY)] * 2,
+        + [pl.BlockSpec(memory_space=pltpu.HBM)] * 2,
         out_specs=[pl.BlockSpec(memory_space=pltpu.VMEM)] * 4,
         scratch_shapes=[
             pltpu.VMEM((3, 64, 1024), bf16),
@@ -461,40 +493,34 @@
         compiler_params=pltpu.CompilerParams(vmem_limit_bytes=16 << 20),
         cost_estimate=pl.CostEstimate(flops=0, bytes_accessed=1 << 20, transcendentals=0),
     )(place, step_sizes[0].T, w_qkv[0], w_out[0].T)
-    key_value, query_out, step_rows = kernel_call(
+    key_value, query_out, step = kernel_call(
         sort_body,
-        [shape(2, 256, 256), shape(2, 256, 256), shape(4, 8, 256, dtype=f32)],
+        [shape(2, 256, 256), shape(2, 256, 256), shape(512, 128, dtype=f32)],
         [place, *to_head_chips(pieces)],
     )
 
     key_value_blocks = ring_gather(key_value, 4, 3)
     query_out_blocks = ring_gather(query_out, 3, 4)
-
-    step_all = step_rows[:, 0, :128] + step_rows[:, 0, 128:]
-    step = jnp.concatenate(
-        [lax.dynamic_index_in_dim(step_all, (y + k) % 4, 0, False) for k in (0, 3, 1, 2)]
-    )[:, None]
 
     tokens, _ = lax.optimization_barrier((group_in[0], pieces[0]))
     turned = kernel_call(turn_body, shape(128, 2048), [place, tokens])
     rows = kernel_call(
         join_body,
         shape(512, 2048),
-        [place, turned] + [moved(turned, "y", hop) for hop in (1, -1, 2)],
-    )
-
-    part = lax.dynamic_slice(momentum[0], (y % 2, 0, z * 64, 0), (1, 3, 64, 512)).reshape(192, 512)
-    scalars = jnp.stack([momentum_decay[0], fast_rate[0]])
-    scalars = lax.dynamic_index_in_dim(scalars, y % 2, 1, False)
-    terms = []
-    for _ in range(3):
-        term = lax.reduce_precision(scalars, 8, 7)
-        terms.append(term)
-        scalars = scalars - term
-    terms = jnp.pad(jnp.concatenate(terms), (0, 2))
-    terms = jnp.broadcast_to(terms[:, None], (8, 512)).astype(bf16)
-    part, terms, _ = lax.optimization_barrier((part, terms, pieces[0]))
-    mine = kernel_call(payload_body, shape(1736, 512), [place, fast_weights[0], part, terms])
+        [place, turned] + [moved(turned, "y", hop) for hop in (-1, 2, 1)],
+    )
+
+    gate, _ = lax.optimization_barrier((momentum_decay[0], pieces[0]))
+    mine = pl.pallas_call(
+        payload_body,
+        name="payload",
+        out_shape=shape(1736, 512),
+        in_specs=[pl.BlockSpec(memory_space=pltpu.SMEM)] * 3 + [pl.BlockSpec(memory_space=pltpu.HBM)] * 2,
+        out_specs=pl.BlockSpec(memory_space=pltpu.VMEM),
+        scratch_shapes=[pltpu.VMEM((3, 64, 512), bf16), pltpu.SemaphoreType.DMA((4,))],
+        compiler_params=pltpu.CompilerParams(vmem_limit_bytes=16 << 20),
+        cost_estimate=pl.CostEstimate(flops=0, bytes_accessed=4 << 20, transcendentals=0),
+    )(place, gate, fast_rate[0], fast_weights[0], momentum[0])
     pairs = [(yy * 2 + yy // 2, yy * 2 + 1 - yy // 2) for yy in range(4)]
     mine_sent = lax.ppermute(mine, ("y", "head"), pairs)
     weights, momentum_own, terms = kernel_call(
@@ -502,8 +528,6 @@
         [shape(3, 512, 512), shape(192, 256, dtype=f32), shape(8, 512, dtype=f32)],
         [place, mine, mine_sent],
     )
-    decay = terms[0, 0] + terms[2, 0] + terms[4, 0]
-    rate = (terms[1, 0] + terms[3, 0] + terms[5, 0]).reshape(1, 1)
 
     pair = kernel_call(
         project_body,
@@ -529,8 +553,9 @@
     to_far = moved(parts[4 - 1], "z", 2)
     to_down = moved(parts[5 - 1], "z", -1)
     near = [moved(parts[1 - 1], "z", 1), moved(parts[7 - 1], "z", -1)]
-    ahead = (parts[2 - 1].astype(f32) + to_up.astype(f32) + to_far.astype(f32)).astype(bf16)
-    behind = (parts[6 - 1].astype(f32) + to_down.astype(f32)).astype(bf16)
+    block = shape(192, 256)
+    ahead = kernel_call(sum_body, block, [place, parts[2 - 1], to_up, to_far])
+    behind = kernel_call(sum_body, block, [place, parts[6 - 1], to_down])
     rows, _ = lax.optimization_barrier((rows, parts[3]))
     query_half, out_own, query_sent = kernel_call(
         query_body,
@@ -540,10 +565,8 @@
         scratch=[pltpu.VMEM((2048, 256), bf16)],
     )
     own_sum, _ = lax.optimization_barrier((own_sum, query_sent))
-    total = own_sum
-    for term in (*near, moved(ahead, "z", 2), moved(behind, "z", -2)):
-        total = total + term.astype(f32)
-    moment = (decay * momentum_own + total).astype(bf16)
+    sums = [*near, moved(ahead, "z", 2), moved(behind, "z", -2)]
+    moment = kernel_call(moment_body, block, [place, own_sum, momentum_own, terms, *sums])
     around = {0: moment, 2: moved(moment, "z", -2), 6: moved(moment, "z", 2)}
     around[1], around[7] = moved(moment, "z", -1), moved(moment, "z", 1)
     around[3], around[5] = moved(around[2], "z", -1), moved(around[6], "z", 1)
@@ -556,7 +579,7 @@
     made_top, made_bottom = kernel_call(
         newton_body,
         [shape(3, 256, 512)] * 2,
-        [place, moment_half, moment_other, weights, rate],
+        [place, moment_half, moment_other, weights, terms],
         flops=2 * 512**3 * 18,
         scratch=[pltpu.VMEM((3, 512, 512), bf16)],
     )

time: 222 us -> 220 us (level)
  Pallas kernels: 43.5 us -> 37 us
  waiting for transfers between devices: 82.1 us -> 87.2 us
  between operations: 4.89 us -> 1.06 us
    pallas_call x13 -> x15, Pallas kernels: 39 us -> 31.7 us  [kernel_call(): pl.pallas_call(body, out_shape=outs, in_specs=[pl.BlockSpec(memory_space=...]
    ppermute x36, waiting for transfers between devices: 79 us -> 82.3 us  [moved(): lax.ppermute(value, axis, [(i, (i + steps) % count) for i in range(count)])]
    unnamed x27 -> x19, local copies, waits for them, and re-layouts: 6.41 us -> 8.11 us
  transfers between devices with their start and end apart: 49 -> 49, of which waited for: 17 -> 18; matrix products, arithmetic and copies ran while one was open for 1% -> 0% of each run, Pallas kernels for 14% -> 10%
where the time goes in v2:
time: 220 us; the launch traced here: 219 us
  waiting for transfers between devices  87.2 us (40%)
  starting transfers between devices  85.4 us (39%)
  Pallas kernels  37 us (17%)
  local copies, waits for them, and re-layouts  8.11 us (4%)
    ppermute x36, waiting for transfers between devices, moved(): lax.ppermute(value, axis, [(i, (i + steps) % count) for i in range(count)])  82.3 us
    ppermute x36, starting transfers between devices, moved(): lax.ppermute(value, axis, [(i, (i + steps) % count) for i in range(count)])  56.3 us
    pallas_call x15, Pallas kernels, kernel_call(): pl.pallas_call(body, out_shape=outs, in_specs=[pl.BlockSpec(memory_space=...  31.7 us
    ppermute x4, starting transfers between devices, to_head_chips(): got.append(lax.ppermute(part, ('y', 'head'), pairs))  11.4 us
    ppermute x2, starting transfers between devices, swapped(): return lax.ppermute(value, 'head', [(0, 1), (1, 0)])  8.33 us
    unnamed x19, local copies, waits for them, and re-layouts  8.11 us
    ppermute x6, starting transfers between devices, along(): lax.ppermute(value, ('y', 'head'), [(a * 2 + c, b * 2 + d) for a, c, b, d...  8.09 us
  transfers between devices with their start and end apart: 49, of which 18 were waited for; matrix products, arithmetic and copies ran while one was open for 0% of the time, Pallas kernels for 10%

profile of v2, /device:TPU:1, one launch (start us, length us, event | category | flops | bytes accessed | tf_op | source)
XLA Modules:
  0.0 218.8 jit_solution(14619156538431565985)
XLA Ops:
  4.3 6.2 %collective-permute-start.3 = (bf16[264,256]{1,0:T(8,128)(2,1)S(1)}, bf16[264,256]{1,0:T(8,128)(2,1)S(1)}, u32[]{:S(2)}, u32[]{:S(2)}) collective-permute-start(bf16[264,256]{1,0:T(8,128)(2,1)S(1)} %get-tuple-element.34), channel_id=1, source_target_pairs={{0,0},{1,4},{2,1},{3,5},{4,2},{5,6},{6,3},{7,7},{8,8},{9,12},{10,9... | collective-permute-start | bytes 405512 | tf_op jit(solution)/shard_map/ppermute | solution.py:463
  24.2 4.0 %collective-permute-start.7 = (bf16[2,256,256]{2,1,0:T(8,128)(2,1)S(1)}, bf16[2,256,256]{2,1,0:T(8,128)(2,1)S(1)}, u32[]{:S(2)}, u32[]{:S(2)}) collective-permute-start(bf16[2,256,256]{2,1,0:T(8,128)(2,1)S(1)} %get-tuple-element.39.refs_0_), channel_id=1, source_target_pairs={{0,56},{8,0},{16,8},{24,16},{32,24},{40,32},{48,40},{56,48},{1,57}... | collective-permute-start | bytes 786440 | tf_op jit(solution)/shard_map/ppermute | solution.py:23
  28.2 5.6 %collective-permute-done.10.refs_7_ = bf16[2,256,256]{2,1,0:T(8,128)(2,1)S(1)} collective-permute-done((bf16[2,256,256]{2,1,0:T(8,128)(2,1)S(1)}, bf16[2,256,256]{2,1,0:T(8,128)(2,1)S(1)}, u32[]{:S(2)}, u32[]{:S(2)}) %collective-permute-start.10) | collective-permute-done | bytes 262176 | tf_op jit(solution)/shard_map/ppermute | solution.py:23
  45.4 5.8 %collective-permute-done.8.refs_2_ = bf16[2,256,256]{2,1,0:T(8,128)(2,1)S(1)} collective-permute-done((bf16[2,256,256]{2,1,0:T(8,128)(2,1)S(1)}, bf16[2,256,256]{2,1,0:T(8,128)(2,1)S(1)}, u32[]{:S(2)}, u32[]{:S(2)}) %collective-permute-start.8) | collective-permute-done | bytes 262176 | tf_op jit(solution)/shard_map/ppermute | solution.py:23
  51.2 3.4 %collective-permute-start.9 = (bf16[2,256,256]{2,1,0:T(8,128)(2,1)S(1)}, bf16[2,256,256]{2,1,0:T(8,128)(2,1)S(1)}, u32[]{:S(2)}, u32[]{:S(2)}) collective-permute-start(bf16[2,256,256]{2,1,0:T(8,128)(2,1)S(1)} %collective-permute-done.8.refs_2_), channel_id=1, source_target_pairs={{0,56},{8,0},{16,8},{24,16},{32,24},{40,32},{48,40},{56,48},{1,57}... | collective-permute-start | bytes 786440 | tf_op jit(solution)/shard_map/ppermute | solution.py:23
  54.6 11.9 %collective-permute-done.2.refs_3_ = bf16[128,2048]{1,0:T(8,128)(2,1)S(1)} collective-permute-done((bf16[128,2048]{1,0:T(8,128)(2,1)S(1)}, bf16[128,2048]{1,0:T(8,128)(2,1)S(1)}, u32[]{:S(2)}, u32[]{:S(2)}) %collective-permute-start.2) | collective-permute-done | bytes 524320 | tf_op jit(solution)/shard_map/ppermute | solution.py:23
  72.9 5.5 %collective-permute-done.16.refs_1_ = bf16[2,256,256]{2,1,0:T(8,128)(2,1)S(1)} collective-permute-done((bf16[2,256,256]{2,1,0:T(8,128)(2,1)S(1)}, bf16[2,256,256]{2,1,0:T(8,128)(2,1)S(1)}, u32[]{:S(2)}, u32[]{:S(2)}) %collective-permute-start.16) | collective-permute-done | bytes 262176 | tf_op jit(solution)/shard_map/ppermute | solution.py:23
  78.5 3.4 %collective-permute-start.17 = (bf16[2,256,256]{2,1,0:T(8,128)(2,1)S(1)}, bf16[2,256,256]{2,1,0:T(8,128)(2,1)S(1)}, u32[]{:S(2)}, u32[]{:S(2)}) collective-permute-start(bf16[2,256,256]{2,1,0:T(8,128)(2,1)S(1)} %collective-permute-done.16.refs_1_), channel_id=1, source_target_pairs={{0,56},{8,0},{16,8},{24,16},{32,24},{40,32},{48,40},{56,48},{1,57}... | collective-permute-start | bytes 786440 | tf_op jit(solution)/shard_map/ppermute | solution.py:23
  81.9 4.7 %collective-permute-done.17.refs_2_ = bf16[2,256,256]{2,1,0:T(8,128)(2,1)S(1)} collective-permute-done((bf16[2,256,256]{2,1,0:T(8,128)(2,1)S(1)}, bf16[2,256,256]{2,1,0:T(8,128)(2,1)S(1)}, u32[]{:S(2)}, u32[]{:S(2)}) %collective-permute-start.17) | collective-permute-done | bytes 262176 | tf_op jit(solution)/shard_map/ppermute | solution.py:23
  86.6 3.4 %collective-permute-start.18 = (bf16[2,256,256]{2,1,0:T(8,128)(2,1)S(1)}, bf16[2,256,256]{2,1,0:T(8,128)(2,1)S(1)}, u32[]{:S(2)}, u32[]{:S(2)}) collective-permute-start(bf16[2,256,256]{2,1,0:T(8,128)(2,1)S(1)} %collective-permute-done.17.refs_2_), channel_id=1, source_target_pairs={{0,56},{8,0},{16,8},{24,16},{32,24},{40,32},{48,40},{56,48},{1,57}... | collective-permute-start | bytes 786440 | tf_op jit(solution)/shard_map/ppermute | solution.py:23
  90.0 3.8 %collective-permute-done.18.refs_3_ = bf16[2,256,256]{2,1,0:T(8,128)(2,1)S(1)} collective-permute-done((bf16[2,256,256]{2,1,0:T(8,128)(2,1)S(1)}, bf16[2,256,256]{2,1,0:T(8,128)(2,1)S(1)}, u32[]{:S(2)}, u32[]{:S(2)}) %collective-permute-start.18) | collective-permute-done | bytes 262176 | tf_op jit(solution)/shard_map/ppermute | solution.py:23
  93.8 3.4 %collective-permute-start.19 = (bf16[2,256,256]{2,1,0:T(8,128)(2,1)S(1)}, bf16[2,256,256]{2,1,0:T(8,128)(2,1)S(1)}, u32[]{:S(2)}, u32[]{:S(2)}) collective-permute-start(bf16[2,256,256]{2,1,0:T(8,128)(2,1)S(1)} %collective-permute-done.18.refs_3_), channel_id=1, source_target_pairs={{0,56},{8,0},{16,8},{24,16},{32,24},{40,32},{48,40},{56,48},{1,57}... | collective-permute-start | bytes 786440 | tf_op jit(solution)/shard_map/ppermute | solution.py:23
  98.1 4.0 %shard_map.100 = (f32[192,256]{1,0:T(8,128)S(1)}, bf16[192,256]{1,0:T(8,128)(2,1)S(1)}, bf16[192,256]{1,0:T(8,128)(2,1)S(1)}, bf16[192,256]{1,0:T(8,128)(2,1)S(1...) custom-call(s32[3]{0:T(128)S(1)} %pad_add_fusion.place, ...), custom_call_target="tpu_custom_call" | custom-call | flops 805306368 | bytes 3932160 | tf_op jit(solution)/shard_map/pallas_call | solution.py:36
  112.6 3.3 %collective-permute-start.29 = (bf16[192,256]{1,0:T(8,128)(2,1)S(1)}, bf16[192,256]{1,0:T(8,128)(2,1)S(1)}, u32[]{:S(2)}, u32[]{:S(2)}) collective-permute-start(bf16[192,256]{1,0:T(8,128)(2,1)S(1)} %shard_map.103), channel_id=1, source_target_pairs={{0,48},{8,56},{16,0},{24,8},{32,16},{40,24},{48,32},{56,40},{1,49}... | collective-permute-start | bytes 294920 | tf_op jit(solution)/shard_map/ppermute | solution.py:23
  118.7 4.1 %collective-permute-start.31 = (bf16[192,256]{1,0:T(8,128)(2,1)S(1)}, bf16[192,256]{1,0:T(8,128)(2,1)S(1)}, u32[]{:S(2)}, u32[]{:S(2)}) collective-permute-start(bf16[192,256]{1,0:T(8,128)(2,1)S(1)} %shard_map.104.refs_0_), channel_id=1, source_target_pairs={{0,48},{8,56},{16,0},{24,8},{32,16},{40,24},{48,32},{56,40},{1,49}... | collective-permute-start | bytes 294920 | tf_op jit(solution)/shard_map/ppermute | solution.py:23
  132.8 4.2 %collective-permute-done.33.refs_4_ = bf16[192,256]{1,0:T(8,128)(2,1)S(1)} collective-permute-done((bf16[192,256]{1,0:T(8,128)(2,1)S(1)}, bf16[192,256]{1,0:T(8,128)(2,1)S(1)}, u32[]{:S(2)}, u32[]{:S(2)}) %collective-permute-start.33) | collective-permute-done | bytes 98336 | tf_op jit(solution)/shard_map/ppermute | solution.py:23
  137.8 7.9 %collective-permute-start.37 = (bf16[3584,256]{1,0:T(8,128)(2,1)S(1)}, bf16[3584,256]{1,0:T(8,128)(2,1)S(1)}, u32[]{:S(2)}, u32[]{:S(2)}) collective-permute-start(bf16[3584,256]{1,0:T(8,128)(2,1)S(1)} %shard_map.105.own), channel_id=1, source_target_pairs={{0,1},{1,0},{2,3},{3,2},{4,5},{5,4},{6,7},{7,6},{8,9},{9,8},{10,11... | collective-permute-start | bytes 5505032 | tf_op jit(solution)/shard_map/ppermute | solution.py:27
  145.7 3.4 %collective-permute-done.37.other = bf16[3584,256]{1,0:T(8,128)(2,1)S(1)} collective-permute-done((bf16[3584,256]{1,0:T(8,128)(2,1)S(1)}, bf16[3584,256]{1,0:T(8,128)(2,1)S(1)}, u32[]{:S(2)}, u32[]{:S(2)}) %collective-permute-start.37) | collective-permute-done | bytes 1835040 | tf_op jit(solution)/shard_map/ppermute | solution.py:27
  149.1 10.9 %shard_map.106 = (bf16[3,256,512]{2,1,0:T(8,128)(2,1)S(1)}, bf16[3,256,512]{2,1,0:T(8,128)(2,1)S(1)}) custom-call(s32[3]{0:T(128)S(1)} %pad_add_fusion.place, bf16[3584,256]{1,0:T(8,128)(2,1)S(1)} %shard_map.105.own, bf16[3584,256]{1,0:T(8,128)(2,1)S(1)} %collective-permute-done.37.other, bf16[3,512,512]{2,1,0:T(8,128)(2,1)S(1)} %get-tuple-element.42.weights, ...), custom_call_target="tpu_custom_call" | custom-call | flops 4831838208 | bytes 5259264 | tf_op jit(solution)/shard_map/pallas_call | solution.py:36
  162.0 5.8 %shard_map.107 = (f32[384,1024]{1,0:T(8,128)S(1)}, bf16[64,1024]{1,0:T(8,128)(2,1)S(1)}, bf16[64,1024]{1,0:T(8,128)(2,1)S(1)}) custom-call(s32[3]{0:T(128)S(1)} %pad_add_fusion.place, f32[512,256]{1,0:T(8,128)S(1)} %get-tuple-element.46.query_own, bf16[1024,256]{1,0:T(8,128)(2,1)S(1)} %get-tuple-element.47.out_own, ...), custom_call_target="tpu_custom_call" | custom-call | flops 1342177280 | bytes 4456448 | tf_op jit(solution)/shard_map/pallas_call | solution.py:36
  167.9 3.4 %collective-permute-start.39 = (bf16[64,1024]{1,0:T(8,128)(2,1)S(1)}, bf16[64,1024]{1,0:T(8,128)(2,1)S(1)}, u32[]{:S(2)}, u32[]{:S(2)}) collective-permute-start(bf16[64,1024]{1,0:T(8,128)(2,1)S(1)} %get-tuple-element.63), channel_id=1, source_target_pairs={{0,6},{2,0},{4,2},{6,4},{1,7},{3,1},{5,3},{7,5},{8,14},{10,8},{12,... | collective-permute-start | bytes 393224 | tf_op jit(solution)/shard_map/ppermute | solution.py:23
  171.3 6.1 %collective-permute-done.38.top = bf16[64,1024]{1,0:T(8,128)(2,1)S(1)} collective-permute-done((bf16[64,1024]{1,0:T(8,128)(2,1)S(1)}, bf16[64,1024]{1,0:T(8,128)(2,1)S(1)}, u32[]{:S(2)}, u32[]{:S(2)}) %collective-permute-start.38) | collective-permute-done | bytes 131104 | tf_op jit(solution)/shard_map/ppermute | solution.py:23
  186.3 21.1 %collective-permute-done.41.high = bf16[128,1024]{1,0:T(8,128)(2,1)S(1)} collective-permute-done((bf16[128,1024]{1,0:T(8,128)(2,1)S(1)}, bf16[128,1024]{1,0:T(8,128)(2,1)S(1)}, u32[]{:S(2)}, u32[]{:S(2)}) %collective-permute-start.41) | collective-permute-done | bytes 262176 | tf_op jit(solution)/shard_map/ppermute | solution.py:23
  209.4 5.3 %collective-permute-done.42 = bf16[1,128,1024]{2,1,0:T(8,128)(2,1)S(1)} collective-permute-done((bf16[1,128,1024]{2,1,0:T(8,128)(2,1)S(1)}, bf16[1,128,1024]{2,1,0:T(8,128)(2,1)S(1)}, u32[]{:S(2)}, u32[]{:S(2)}) %collective-permute-start.42) | collective-permute-done | bytes 262176 | tf_op jit(solution)/shard_map/ppermute | solution.py:23
  (113 shorter events, 76.9 us)
Async XLA Ops:
  4.3 16.0 %collective-permute-start.3 = (bf16[264,256]{1,0:T(8,128)(2,1)S(1)}, bf16[264,256]{1,0:T(8,128)(2,1)S(1)}, u32[]{:S(2)}, u32[]{:S(2)}) collective-permute-start(bf16[264,256]{1,0:T(8,128)(2,1)S(1)} %get-tuple-element.34), channel_id=1, source_target_pairs={{0,0},{1,4},{2,1},{3,5},{4,2},{5,6},{6,3},{7,7},{8,8},{9,12},{10,9... | collective-permute-start | bytes 405512 | tf_op jit(solution)/shard_map/ppermute | solution.py:463
  10.5 9.7 %collective-permute-start.4 = (bf16[264,256]{1,0:T(8,128)(2,1)S(1)}, bf16[264,256]{1,0:T(8,128)(2,1)S(1)}, u32[]{:S(2)}, u32[]{:S(2)}) collective-permute-start(bf16[264,256]{1,0:T(8,128)(2,1)S(1)} %get-tuple-element.36), channel_id=1, source_target_pairs={{0,1},{1,5},{2,2},{3,6},{4,3},{5,7},{6,0},{7,4},{8,9},{9,13},{10,1... | collective-permute-start | bytes 405512 | tf_op jit(solution)/shard_map/ppermute | solution.py:463
  17.4 25.0 %collective-permute-start = (bf16[128,2048]{1,0:T(8,128)(2,1)S(1)}, bf16[128,2048]{1,0:T(8,128)(2,1)S(1)}, u32[]{:S(2)}, u32[]{:S(2)}) collective-permute-start(bf16[128,2048]{1,0:T(8,128)(2,1)S(1)} %shard_map.95.refs_0_), channel_id=1, source_target_pairs={{0,6},{2,0},{4,2},{6,4},{1,7},{3,1},{5,3},{7,5},{8,14},{10,8},{12,... | collective-permute-start | bytes 1572872 | tf_op jit(solution)/shard_map/ppermute | solution.py:23
  22.4 11.4 %collective-permute-start.10 = (bf16[2,256,256]{2,1,0:T(8,128)(2,1)S(1)}, bf16[2,256,256]{2,1,0:T(8,128)(2,1)S(1)}, u32[]{:S(2)}, u32[]{:S(2)}) collective-permute-start(bf16[2,256,256]{2,1,0:T(8,128)(2,1)S(1)} %get-tuple-element.39.refs_0_), channel_id=1, source_target_pairs={{0,8},{8,16},{16,24},{24,32},{32,40},{40,48},{48,56},{56,0},{1,9},... | collective-permute-start | bytes 786440 | tf_op jit(solution)/shard_map/ppermute | solution.py:23
  24.2 17.5 %collective-permute-start.7 = (bf16[2,256,256]{2,1,0:T(8,128)(2,1)S(1)}, bf16[2,256,256]{2,1,0:T(8,128)(2,1)S(1)}, u32[]{:S(2)}, u32[]{:S(2)}) collective-permute-start(bf16[2,256,256]{2,1,0:T(8,128)(2,1)S(1)} %get-tuple-element.39.refs_0_), channel_id=1, source_target_pairs={{0,56},{8,0},{16,8},{24,16},{32,24},{40,32},{48,40},{56,48},{1,57}... | collective-permute-start | bytes 786440 | tf_op jit(solution)/shard_map/ppermute | solution.py:23
  33.8 11.5 %collective-permute-start.11 = (bf16[2,256,256]{2,1,0:T(8,128)(2,1)S(1)}, bf16[2,256,256]{2,1,0:T(8,128)(2,1)S(1)}, u32[]{:S(2)}, u32[]{:S(2)}) collective-permute-start(bf16[2,256,256]{2,1,0:T(8,128)(2,1)S(1)} %collective-permute-done.10.refs_7_), channel_id=1, source_target_pairs={{0,8},{8,16},{16,24},{24,32},{32,40},{40,48},{48,56},{56,0},{1,9},... | collective-permute-start | bytes 786440 | tf_op jit(solution)/shard_map/ppermute | solution.py:23
  38.4 58.8 %collective-permute-start.15 = (bf16[1736,512]{1,0:T(8,128)(2,1)S(1)}, bf16[1736,512]{1,0:T(8,128)(2,1)S(1)}, u32[]{:S(2)}, u32[]{:S(2)}) collective-permute-start(bf16[1736,512]{1,0:T(8,128)(2,1)S(1)} %payload.1.mine), channel_id=1, source_target_pairs={{0,1},{2,3},{5,4},{7,6},{8,9},{10,11},{13,12},{15,14},{16,17},{18,... | collective-permute-start | bytes 5333000 | tf_op jit(solution)/shard_map/ppermute | solution.py:525
  39.7 14.8 %collective-permute-start.1 = (bf16[128,2048]{1,0:T(8,128)(2,1)S(1)}, bf16[128,2048]{1,0:T(8,128)(2,1)S(1)}, u32[]{:S(2)}, u32[]{:S(2)}) collective-permute-start(bf16[128,2048]{1,0:T(8,128)(2,1)S(1)} %shard_map.95.refs_0_), channel_id=1, source_target_pairs={{0,4},{2,6},{4,0},{6,2},{1,5},{3,7},{5,1},{7,3},{8,12},{10,14},{12... | collective-permute-start | bytes 1572872 | tf_op jit(solution)/shard_map/ppermute | solution.py:23
  41.6 24.9 %collective-permute-start.2 = (bf16[128,2048]{1,0:T(8,128)(2,1)S(1)}, bf16[128,2048]{1,0:T(8,128)(2,1)S(1)}, u32[]{:S(2)}, u32[]{:S(2)}) collective-permute-start(bf16[128,2048]{1,0:T(8,128)(2,1)S(1)} %shard_map.95.refs_0_), channel_id=1, source_target_pairs={{0,2},{2,4},{4,6},{6,0},{1,3},{3,5},{5,7},{7,1},{8,10},{10,12},{12... | collective-permute-start | bytes 1572872 | tf_op jit(solution)/shard_map/ppermute | solution.py:23
  51.2 16.1 %collective-permute-start.9 = (bf16[2,256,256]{2,1,0:T(8,128)(2,1)S(1)}, bf16[2,256,256]{2,1,0:T(8,128)(2,1)S(1)}, u32[]{:S(2)}, u32[]{:S(2)}) collective-permute-start(bf16[2,256,256]{2,1,0:T(8,128)(2,1)S(1)} %collective-permute-done.8.refs_2_), channel_id=1, source_target_pairs={{0,56},{8,0},{16,8},{24,16},{32,24},{40,32},{48,40},{56,48},{1,57}... | collective-permute-start | bytes 786440 | tf_op jit(solution)/shard_map/ppermute | solution.py:23
  54.6 12.7 %collective-permute-start.13 = (bf16[2,256,256]{2,1,0:T(8,128)(2,1)S(1)}, bf16[2,256,256]{2,1,0:T(8,128)(2,1)S(1)}, u32[]{:S(2)}, u32[]{:S(2)}) collective-permute-start(bf16[2,256,256]{2,1,0:T(8,128)(2,1)S(1)} %collective-permute-done.12.refs_5_), channel_id=1, source_target_pairs={{0,8},{8,16},{16,24},{24,32},{32,40},{40,48},{48,56},{56,0},{1,9},... | collective-permute-start | bytes 786440 | tf_op jit(solution)/shard_map/ppermute | solution.py:23
  69.8 28.3 %collective-permute-start.14 = (f32[1024,256]{1,0:T(8,128)S(1)}, f32[1024,256]{1,0:T(8,128)S(1)}, u32[]{:S(2)}, u32[]{:S(2)}) collective-permute-start(f32[1024,256]{1,0:T(8,128)S(1)} %shard_map.98.pair_own), channel_id=1, source_target_pairs={{0,1},{1,0},{2,3},{3,2},{4,5},{5,4},{6,7},{7,6},{8,9},{9,8},{10,11... | collective-permute-start | bytes 3145736 | tf_op jit(solution)/shard_map/ppermute | solution.py:27
  90.0 22.6 %collective-permute-start.22 = (bf16[2,256,256]{2,1,0:T(8,128)(2,1)S(1)}, bf16[2,256,256]{2,1,0:T(8,128)(2,1)S(1)}, u32[]{:S(2)}, u32[]{:S(2)}) collective-permute-start(bf16[2,256,256]{2,1,0:T(8,128)(2,1)S(1)} %collective-permute-done.21.refs_6_), channel_id=1, source_target_pairs={{0,8},{8,16},{16,24},{24,32},{32,40},{40,48},{48,56},{56,0},{1,9},... | collective-permute-start | bytes 786440 | tf_op jit(solution)/shard_map/ppermute | solution.py:23
  93.8 22.1 %collective-permute-start.19 = (bf16[2,256,256]{2,1,0:T(8,128)(2,1)S(1)}, bf16[2,256,256]{2,1,0:T(8,128)(2,1)S(1)}, u32[]{:S(2)}, u32[]{:S(2)}) collective-permute-start(bf16[2,256,256]{2,1,0:T(8,128)(2,1)S(1)} %collective-permute-done.18.refs_3_), channel_id=1, source_target_pairs={{0,56},{8,0},{16,8},{24,16},{32,24},{40,32},{48,40},{56,48},{1,57}... | collective-permute-start | bytes 786440 | tf_op jit(solution)/shard_map/ppermute | solution.py:23
  106.9 10.8 %collective-permute-start.23 = (bf16[192,256]{1,0:T(8,128)(2,1)S(1)}, bf16[192,256]{1,0:T(8,128)(2,1)S(1)}, u32[]{:S(2)}, u32[]{:S(2)}) collective-permute-start(bf16[192,256]{1,0:T(8,128)(2,1)S(1)} %get-tuple-element.53), channel_id=1, source_target_pairs={{0,8},{8,16},{16,24},{24,32},{32,40},{40,48},{48,56},{56,0},{1,9},... | collective-permute-start | bytes 294920 | tf_op jit(solution)/shard_map/ppermute | solution.py:23
  137.8 11.3 %collective-permute-start.37 = (bf16[3584,256]{1,0:T(8,128)(2,1)S(1)}, bf16[3584,256]{1,0:T(8,128)(2,1)S(1)}, u32[]{:S(2)}, u32[]{:S(2)}) collective-permute-start(bf16[3584,256]{1,0:T(8,128)(2,1)S(1)} %shard_map.105.own), channel_id=1, source_target_pairs={{0,1},{1,0},{2,3},{3,2},{4,5},{5,4},{6,7},{7,6},{8,9},{9,8},{10,11... | collective-permute-start | bytes 5505032 | tf_op jit(solution)/shard_map/ppermute | solution.py:27
  160.0 20.8 %collective-permute-start.43 = (bf16[3,256,512]{2,1,0:T(8,128)(2,1)S(1)}, bf16[3,256,512]{2,1,0:T(8,128)(2,1)S(1)}, u32[]{:S(2)}, u32[]{:S(2)}) collective-permute-start(bf16[3,256,512]{2,1,0:T(8,128)(2,1)S(1)} %get-tuple-element.59.upper.made_top), channel_id=1, source_target_pairs={{0,2},{2,0},{5,7},{7,5},{8,10},{10,8},{13,15},{15,13},{16,18},{18,... | collective-permute-start | bytes 2359304 | tf_op jit(solution)/shard_map/ppermute | solution.py:588
  160.7 21.3 %collective-permute-start.45 = (bf16[3,256,512]{2,1,0:T(8,128)(2,1)S(1)}, bf16[3,256,512]{2,1,0:T(8,128)(2,1)S(1)}, u32[]{:S(2)}, u32[]{:S(2)}) collective-permute-start(bf16[3,256,512]{2,1,0:T(8,128)(2,1)S(1)} %get-tuple-element.60.lower.made_bottom), channel_id=1, source_target_pairs={{2,4},{0,6},{7,1},{5,3},{10,12},{8,14},{15,9},{13,11},{18,20},{16,... | collective-permute-start | bytes 2359304 | tf_op jit(solution)/shard_map/ppermute | solution.py:588
  167.8 9.7 %collective-permute-start.38 = (bf16[64,1024]{1,0:T(8,128)(2,1)S(1)}, bf16[64,1024]{1,0:T(8,128)(2,1)S(1)}, u32[]{:S(2)}, u32[]{:S(2)}) collective-permute-start(bf16[64,1024]{1,0:T(8,128)(2,1)S(1)} %get-tuple-element.62), channel_id=1, source_target_pairs={{0,2},{2,4},{4,6},{6,0},{1,3},{3,5},{5,7},{7,1},{8,10},{10,12},{12... | collective-permute-start | bytes 393224 | tf_op jit(solution)/shard_map/ppermute | solution.py:23
  178.7 35.9 %collective-permute-start.47 = (bf16[3,256,512]{2,1,0:T(8,128)(2,1)S(1)}, bf16[3,256,512]{2,1,0:T(8,128)(2,1)S(1)}, u32[]{:S(2)}, u32[]{:S(2)}) collective-permute-start(bf16[3,256,512]{2,1,0:T(8,128)(2,1)S(1)} %get-tuple-element.60.lower.made_bottom), channel_id=1, source_target_pairs={{0,2},{2,0},{5,7},{7,5},{8,10},{10,8},{13,15},{15,13},{16,18},{18,... | collective-permute-start | bytes 2359304 | tf_op jit(solution)/shard_map/ppermute | solution.py:588
  179.4 35.2 %collective-permute-start.48 = (bf16[3,256,512]{2,1,0:T(8,128)(2,1)S(1)}, bf16[3,256,512]{2,1,0:T(8,128)(2,1)S(1)}, u32[]{:S(2)}, u32[]{:S(2)}) collective-permute-start(bf16[3,256,512]{2,1,0:T(8,128)(2,1)S(1)} %get-tuple-element.59.upper.made_top), channel_id=1, source_target_pairs={{2,4},{0,6},{7,1},{5,3},{10,12},{8,14},{15,9},{13,11},{18,20},{16,... | collective-permute-start | bytes 2359304 | tf_op jit(solution)/shard_map/ppermute | solution.py:588
  180.7 35.7 %collective-permute-start.44 = (bf16[3,256,512]{2,1,0:T(8,128)(2,1)S(1)}, bf16[3,256,512]{2,1,0:T(8,128)(2,1)S(1)}, u32[]{:S(2)}, u32[]{:S(2)}) collective-permute-start(bf16[3,256,512]{2,1,0:T(8,128)(2,1)S(1)} %collective-permute-done.43.across_top), channel_id=1, source_target_pairs={{2,4},{0,6},{7,1},{5,3},{10,12},{8,14},{15,9},{13,11},{18,20},{16,... | collective-permute-start | bytes 2359304 | tf_op jit(solution)/shard_map/ppermute | solution.py:588
  182.0 34.4 %collective-permute-start.46 = (bf16[3,256,512]{2,1,0:T(8,128)(2,1)S(1)}, bf16[3,256,512]{2,1,0:T(8,128)(2,1)S(1)}, u32[]{:S(2)}, u32[]{:S(2)}) collective-permute-start(bf16[3,256,512]{2,1,0:T(8,128)(2,1)S(1)} %collective-permute-done.45.outward_bottom), channel_id=1, source_target_pairs={{1,3},{3,1},{4,6},{6,4},{9,11},{11,9},{12,14},{14,12},{17,19},{19,... | collective-permute-start | bytes 2359304 | tf_op jit(solution)/shard_map/ppermute | solution.py:588
  186.3 21.1 %collective-permute-start.41 = (bf16[128,1024]{1,0:T(8,128)(2,1)S(1)}, bf16[128,1024]{1,0:T(8,128)(2,1)S(1)}, u32[]{:S(2)}, u32[]{:S(2)}) collective-permute-start(bf16[128,1024]{1,0:T(8,128)(2,1)S(1)} %get-tuple-element.65), channel_id=1, source_target_pairs={{0,2},{2,4},{4,6},{6,0},{1,3},{3,5},{5,7},{7,1},{8,10},{10,12},{12... | collective-permute-start | bytes 786440 | tf_op jit(solution)/shard_map/ppermute | solution.py:23
  (34 other events, 300.1 us)
